TPU v7x, 32 devices: a whole 2x2x4 slice. The times are simulated.
32 devices in a mesh: ctx: 4 (over x, core), seq: 8 (over z, y).
Axes of the slice: x: 2, y: 2, z: 4, core: 2. Of those that a mesh axis runs over, the one named last changes fastest.
Arguments:
- queries: bfloat16 [6144, 1024], P(('seq', 'ctx')), parts along dimension 0, may hold values from -6 to 6
- key_vectors: bfloat16 [6144, 128], P(('seq', 'ctx')), parts along dimension 0, may hold values from -4 to 4
- value_vectors: bfloat16 [6144, 128], P(('seq', 'ctx')), parts along dimension 0, may hold values from -6 to 6
- out_grad: bfloat16 [6144, 1024], P(('seq', 'ctx')), parts along dimension 0, may hold values from -6 to 6
- span_order: int32 [64], P('seq'), parts along dimension 0, may hold values from 0 to 7, each once
- doc_lengths: int32 [48], P('seq'), parts along dimension 0, may hold values from 1 to 256, 768 in all
Outputs:
- attended: bfloat16 [6144, 1024], P(('seq', 'ctx')), parts along dimension 0
- query_grad: bfloat16 [6144, 1024], P(('seq', 'ctx')), parts along dimension 0
- key_grad: bfloat16 [6144, 128], P(('seq', 'ctx')), parts along dimension 0
- value_grad: bfloat16 [6144, 128], P(('seq', 'ctx')), parts along dimension 0
There are 8 independent parts, one for each index of `seq`. A program takes and returns all parts, laid end to end along the dimension named above; each array names one. Nothing has to cross between parts.
Inputs may be any that keep to these rules, and one draw needn't show every extreme that they name: `span_order`: each of 0 to 7 appears once. `doc_lengths`: the lengths sum to 768.
All inputs are finite; a program needn't handle non-finite values.
Results may differ from a plain program's by a relative error of at most 0.015.
Values may be sent and summed in bfloat16 or wider, within the bound.
No kernel may reach another device: no remote copies, remote signals or barrier semaphores. Data moves between devices by JAX's collectives and lax.ppermute only.
A program may use at most 64 MiB of HBM per device.

v0:
```python
import math

import jax
import jax.numpy as jnp
from jax import lax
from jax.sharding import PartitionSpec as P

HQ = 8
DH = 128


negative_fill = -1e30


def from_behind(block, axis, distance):
    devices = range(lax.axis_size(axis))
    route = [((i - distance) % len(devices), i) for i in devices]
    return lax.ppermute(block, axis, route)


def over_blocks(update, running, pieces, offset):
    row_count = pieces[0].shape[0]
    block_keys = 256
    if row_count > block_keys and row_count % block_keys == 0:
        stacked = tuple(
            (piece.reshape(row_count // block_keys, block_keys, piece.shape[1]) for piece in pieces)
        )

        def advance(state_in, element):
            sub_block, number = element
            return (update(state_in, sub_block, number * block_keys), None)

        running, unused = lax.scan(
            advance, running, (stacked, jnp.arange(row_count // block_keys, dtype=jnp.int32))
        )
        return running
    return update(running, pieces, offset)


def unchanged(state_in):
    return state_in


def local(queries, key_vectors, value_vectors, out_grad, span_order, doc_lengths):
    tok_rows = queries.shape[0]
    ctx_count = lax.axis_size("ctx")
    own_index = lax.axis_index("ctx")
    seq_len = tok_rows * ctx_count
    span_rows = seq_len // span_order.shape[0]
    score_scale = 1.0 / math.sqrt(DH)
    offsets = jnp.arange(span_rows, dtype=jnp.int32)
    positions = (span_order[:, None] * span_rows + offsets[None, :]).reshape(seq_len)
    doc_ends = jnp.cumsum(doc_lengths)
    documents = jnp.sum((positions[:, None] >= doc_ends[None, :]).astype(jnp.int32), axis=1)
    own_start = own_index * tok_rows
    query_pos = lax.dynamic_slice_in_dim(positions, own_start, tok_rows, 0)
    query_doc = lax.dynamic_slice_in_dim(documents, own_start, tok_rows, 0)
    query_flat = queries.reshape(tok_rows * HQ, DH)
    grads_out = out_grad.reshape(tok_rows * HQ, DH)

    def visible(offset, row_count):
        key_pos = lax.dynamic_slice_in_dim(positions, offset, row_count, 0)
        key_doc = lax.dynamic_slice_in_dim(documents, offset, row_count, 0)
        return (query_doc[:, None] == key_doc[None, :]) & (key_pos[None, :] <= query_pos[:, None])

    def logits(key_rows):
        scores = lax.dot_general(
            query_flat, key_rows, (((1,), (1,)), ((), ())), preferred_element_type=jnp.float32
        )
        return (scores * score_scale).reshape(tok_rows, HQ, key_rows.shape[0])

    def forward_step(running, pieces, offset):
        key_rows, value_rows = pieces
        row_count = key_rows.shape[0]
        allowed = visible(offset, row_count)

        def forward_active(state_in):
            row_max, row_sum, accumulated = state_in
            mask_wide = allowed[:, None, :]
            scores = jnp.where(mask_wide, logits(key_rows), negative_fill)
            new_max = jnp.maximum(row_max, jnp.max(scores, axis=-1).reshape(-1))
            weights = jnp.where(mask_wide, jnp.exp(scores - new_max.reshape(tok_rows, HQ, 1)), 0.0)
            weights = weights.reshape(tok_rows * HQ, row_count)
            rescale = jnp.exp(row_max - new_max)
            row_sum = row_sum * rescale + jnp.sum(weights, axis=-1)
            accumulated = accumulated * rescale[:, None] + jnp.dot(
                weights.astype(jnp.bfloat16), value_rows, preferred_element_type=jnp.float32
            )
            return (new_max, row_sum, accumulated)

        return lax.cond(jnp.any(allowed), forward_active, unchanged, running)

    start_state = (
        jnp.full((tok_rows * HQ,), negative_fill, jnp.float32),
        jnp.zeros((tok_rows * HQ,), jnp.float32),
        jnp.zeros((tok_rows * HQ, DH), jnp.float32),
    )
    row_max, row_sum, accumulated = over_blocks(
        forward_step,
        start_state,
        (
            lax.all_gather(key_vectors, "ctx", axis=0, tiled=True),
            lax.all_gather(value_vectors, "ctx", axis=0, tiled=True),
        ),
        jnp.int32(0),
    )
    attended = (accumulated / row_sum[:, None]).astype(jnp.bfloat16)
    log_norm = row_max + jnp.log(row_sum)
    out_float = lax.optimization_barrier(attended).astype(jnp.float32)
    row_dots = jnp.sum(grads_out.astype(jnp.float32) * out_float, axis=-1)

    def backward_updater():

        def update(running, pieces, offset):
            key_rows, value_rows = pieces
            row_count = key_rows.shape[0]
            allowed = visible(offset, row_count)

            def update_active(state_in):
                query_acc, key_acc, value_acc = state_in
                mask_wide = allowed[:, None, :]
                weights = jnp.where(
                    mask_wide, jnp.exp(logits(key_rows) - log_norm.reshape(tok_rows, HQ, 1)), 0.0
                )
                weights = weights.reshape(tok_rows * HQ, row_count)
                value_part = lax.dot_general(
                    weights.astype(jnp.bfloat16),
                    grads_out,
                    (((0,), (0,)), ((), ())),
                    preferred_element_type=jnp.float32,
                )
                weight_grads = lax.dot_general(
                    grads_out,
                    value_rows,
                    (((1,), (1,)), ((), ())),
                    preferred_element_type=jnp.float32,
                )
                score_grads = (weights * (weight_grads - row_dots[:, None])).astype(jnp.bfloat16)
                query_acc = query_acc + jnp.dot(
                    score_grads, key_rows, preferred_element_type=jnp.float32
                )
                key_part = lax.dot_general(
                    score_grads,
                    query_flat,
                    (((0,), (0,)), ((), ())),
                    preferred_element_type=jnp.float32,
                )
                key_acc = key_acc + key_part
                value_acc = value_acc + value_part
                return (query_acc, key_acc, value_acc)

            return lax.cond(jnp.any(allowed), update_active, unchanged, running)

        return update

    query_zero = jnp.zeros((tok_rows * HQ, DH), jnp.float32)

    def pass_grads(key_acc, value_acc):
        return (
            from_behind(key_acc.astype(jnp.bfloat16), "ctx", 1).astype(key_acc.dtype),
            from_behind(value_acc.astype(jnp.bfloat16), "ctx", 1).astype(value_acc.dtype),
        )

    def one_turn(turn_index, state_in):
        key_rows, value_rows, query_acc, key_acc, value_acc = state_in
        anchor = (own_index - turn_index) % ctx_count
        offset = anchor * tok_rows
        query_acc, key_acc, value_acc = over_blocks(
            backward_updater(), (query_acc, key_acc, value_acc), (key_rows, value_rows), offset
        )
        return (key_rows, value_rows, query_acc, key_acc, value_acc)

    def cycle_turn(turn_index, state_in):
        key_rows, value_rows, query_acc, key_acc, value_acc = one_turn(turn_index, state_in)
        key_rows, value_rows = from_behind((key_rows, value_rows), "ctx", 1)
        key_acc, value_acc = pass_grads(key_acc, value_acc)
        return (key_rows, value_rows, query_acc, key_acc, value_acc)

    shard_zero = jnp.zeros((tok_rows, DH), jnp.float32)
    state_now = lax.fori_loop(
        0,
        ctx_count - 1,
        cycle_turn,
        (key_vectors, value_vectors, query_zero, shard_zero, shard_zero),
    )
    state_now = one_turn(ctx_count - 1, state_now)
    query_acc = state_now[2]
    key_acc, value_acc = pass_grads(state_now[3], state_now[4])
    query_grad = (query_acc * score_scale).astype(jnp.bfloat16).reshape(tok_rows, HQ * DH)
    key_grad = (key_acc * score_scale).astype(jnp.bfloat16)
    value_grad = value_acc.astype(jnp.bfloat16)
    return (attended.reshape(tok_rows, HQ * DH), query_grad, key_grad, value_grad)


def solution(mesh):
    in_specs = (
        P(("seq", "ctx"), None),
        P(("seq", "ctx"), None),
        P(("seq", "ctx"), None),
        P(("seq", "ctx"), None),
        P("seq"),
        P("seq"),
    )
    out_specs = (
        P(("seq", "ctx"), None),
        P(("seq", "ctx"), None),
        P(("seq", "ctx"), None),
        P(("seq", "ctx"), None),
    )
    return jax.shard_map(local, mesh=mesh, in_specs=in_specs, out_specs=out_specs, check_vma=False)
```

profile of v0, /device:TPU:0, one launch (start us, length us, event | category | flops | bytes accessed | tf_op | source)
XLA Modules:
  0.0 70.6 jit_solution(5478029495686543589)
XLA Ops:
  0.6 0.8 %copy.78 = bf16[192,128]{1,0:T(8,128)(2,1)S(1)} copy(bf16[192,128]{1,0:T(8,128)(2,1)} %param.18) | data formatting | bytes 98304
  1.4 0.8 %copy.77 = bf16[192,128]{1,0:T(8,128)(2,1)S(1)} copy(bf16[192,128]{1,0:T(8,128)(2,1)} %param.17) | data formatting | bytes 98304
  3.0 0.8 %reduce-window.8 = s32[6,1]{0,1:T(1,128)S(1)} reduce-window(s32[6,1]{0,1:T(1,128)} %bitcast.47, s32[]{:T(128)} %constant.146.clone.1), window={size=6x1 pad=5_0x0_0}, to_apply=%region_0.0 | reduce-window | flops 30 | bytes 52 | tf_op jit(solution)/shard_map/reduce-window.3
  3.9 1.2 %reshape.121 = bf16[1536,128]{1,0:T(8,128)(2,1)S(1)} reshape(bf16[192,1024]{1,0:T(8,128)(2,1)} %param.16) | data formatting | bytes 786432 | tf_op jit(solution)/shard_map/reshape | solution.py:58
  5.0 6.9 %all_gather.7 = bf16[768,128]{1,0:T(8,128)(2,1)S(1)} all-gather(bf16[192,128]{1,0:T(8,128)(2,1)S(1)} %copy.78), channel_id=1, replica_groups=mesh['ctx'=4,'seq'=8] {'ctx'}, dimensions={0}, use_global_device_ids=true | all-gather | bytes 245760 | tf_op jit(solution)/shard_map/all_gather | solution.py:103
  11.9 5.6 %all_gather.6 = bf16[768,128]{1,0:T(8,128)(2,1)S(1)} all-gather(bf16[192,128]{1,0:T(8,128)(2,1)S(1)} %copy.77), channel_id=1, replica_groups=mesh['ctx'=4,'seq'=8] {'ctx'}, dimensions={0}, use_global_device_ids=true | all-gather | bytes 245760 | tf_op jit(solution)/shard_map/all_gather | solution.py:102
  17.7 15.5 %while.38 = (s32[]{:T(128)}, f32[1536]{0:T(1024)S(1)}, f32[1536]{0:T(1024)S(1)}, f32[1536,128]{1,0:T(8,128)S(1)}, s32[192]{0:T(256)S(1)}, /*index=5*/s32[3]{0:T(...) while((s32[]{:T(128)}, f32[1536]{0:T(1024)S(1)}, ...), condition=%wide.region_8.9_spmd, body=%wide.region_2.8_spmd.sunk | while | flops 205458432 | bytes 9383773 | solution.py:33
  20.5 2.4 %conditional.7 = ((f32[1536]{0:T(1024)S(1)}, f32[1536]{0:T(1024)S(1)}, f32[1536,128]{1,0:T(8,128)S(1)})) conditional(s32[]{:T(128)} %convert_element_type.138, (f32[1536]{0:T(1024)S(1)}, f32[1536]{0:T(1024)S(1)}, f32[1536,128]{1,0:T(8,128)S(1)}) %tuple.103, (pred[192,256]{1,0:T(8,128)(4,1)S(1)}, bf16[3,256,128]{2,1,0:T(8,128)(2,1)S(1)}, s32[]{:T(128)}, ...), branch_computations={%region_4.4_spmd, %region_5.7_spmd} | conditional | flops 205261824 | bytes 9326632 | solution.py:91
  22.1 0.8 %convolution_add_fusion = f32[1536,128]{1,0:T(8,128)S(1)} fusion(pred[1536,256]{0,1:T(32,128)(4,1)S(1)} %copy.14, f32[1536,256]{0,1:T(8,128)S(1)} %get-tuple-element.709, f32[1536,128]{1,0:T(8,128)S(1)} %get-tuple-element.512, f32[1536]{0:T(1024)S(1)} %max.4, f32[1536]{0:T(1024)S(1)} %get-tuple-element.701, bf16[3,256,128]{2,1,0:T(8,128)(2,1)S(1)} %get-tuple-element.513, ...), kind=kOutput, calls=%fused_computation.3 | convolution fusion | flops 102236160 | bytes 3620868 | tf_op jit(solution)/shard_map/while/body/eval_jaxpr/cond/branch_1_fun/dot_general | solution.py:86
  25.7 2.4 %conditional.7 = ((f32[1536]{0:T(1024)S(1)}, f32[1536]{0:T(1024)S(1)}, f32[1536,128]{1,0:T(8,128)S(1)})) conditional(s32[]{:T(128)} %convert_element_type.138, (f32[1536]{0:T(1024)S(1)}, f32[1536]{0:T(1024)S(1)}, f32[1536,128]{1,0:T(8,128)S(1)}) %tuple.103, (pred[192,256]{1,0:T(8,128)(4,1)S(1)}, bf16[3,256,128]{2,1,0:T(8,128)(2,1)S(1)}, s32[]{:T(128)}, ...), branch_computations={%region_4.4_spmd, %region_5.7_spmd} | conditional | flops 205261824 | bytes 9326632 | solution.py:91
  27.3 0.8 %convolution_add_fusion = f32[1536,128]{1,0:T(8,128)S(1)} fusion(pred[1536,256]{0,1:T(32,128)(4,1)S(1)} %copy.14, f32[1536,256]{0,1:T(8,128)S(1)} %get-tuple-element.709, f32[1536,128]{1,0:T(8,128)S(1)} %get-tuple-element.512, f32[1536]{0:T(1024)S(1)} %max.4, f32[1536]{0:T(1024)S(1)} %get-tuple-element.701, bf16[3,256,128]{2,1,0:T(8,128)(2,1)S(1)} %get-tuple-element.513, ...), kind=kOutput, calls=%fused_computation.3 | convolution fusion | flops 102236160 | bytes 3620868 | tf_op jit(solution)/shard_map/while/body/eval_jaxpr/cond/branch_1_fun/dot_general | solution.py:86
  30.9 2.4 %conditional.7 = ((f32[1536]{0:T(1024)S(1)}, f32[1536]{0:T(1024)S(1)}, f32[1536,128]{1,0:T(8,128)S(1)})) conditional(s32[]{:T(128)} %convert_element_type.138, (f32[1536]{0:T(1024)S(1)}, f32[1536]{0:T(1024)S(1)}, f32[1536,128]{1,0:T(8,128)S(1)}) %tuple.103, (pred[192,256]{1,0:T(8,128)(4,1)S(1)}, bf16[3,256,128]{2,1,0:T(8,128)(2,1)S(1)}, s32[]{:T(128)}, ...), branch_computations={%region_4.4_spmd, %region_5.7_spmd} | conditional | flops 205261824 | bytes 9326632 | solution.py:91
  32.4 0.8 %convolution_add_fusion = f32[1536,128]{1,0:T(8,128)S(1)} fusion(pred[1536,256]{0,1:T(32,128)(4,1)S(1)} %copy.14, f32[1536,256]{0,1:T(8,128)S(1)} %get-tuple-element.709, f32[1536,128]{1,0:T(8,128)S(1)} %get-tuple-element.512, f32[1536]{0:T(1024)S(1)} %max.4, f32[1536]{0:T(1024)S(1)} %get-tuple-element.701, bf16[3,256,128]{2,1,0:T(8,128)(2,1)S(1)} %get-tuple-element.513, ...), kind=kOutput, calls=%fused_computation.3 | convolution fusion | flops 102236160 | bytes 3620868 | tf_op jit(solution)/shard_map/while/body/eval_jaxpr/cond/branch_1_fun/dot_general | solution.py:86
  34.5 0.8 %fusion.28 = (pred[]{:T(512)}, pred[192,192]{1,0:T(8,128)(4,1)S(1)}) fusion(s32[192]{0:T(256)S(1)} %get-tuple-element.1069, s32[192]{0:T(256)S(1)} %get-tuple-element.717, s32[192]{0:T(256)S(1)} %get-tuple-element.712, s32[192]{0:T(256)S(1)} %get-tuple-element.1068), kind=kLoop, calls=%fused_computation.58 | loop fusion | flops 147455 | bytes 39937 | tf_op jit(solution)/shard_map/reduce_or | solution.py:152
  36.2 28.9 %while.39 = (s32[]{:T(128)}, bf16[192,128]{1,0:T(8,128)(2,1)S(1)}, bf16[192,128]{1,0:T(8,128)(2,1)S(1)}, f32[1536,128]{1,0:T(8,128)S(1)}, f32[192,128]{1,0:T(8,1...) while((s32[]{:T(128)}, bf16[192,128]{1,0:T(8,128)(2,1)S(1)}, ...), condition=%wide.region_15.16_spmd.clone, body=%wide.region_11.15_spmd.clone.sunk | while | flops 380092448 | bytes 12233380 | solution.py:180
  36.4 0.8 %fusion.54 = (pred[]{:T(512)}, pred[192,192]{1,0:T(8,128)(4,1)S(1)}) fusion(s32[192]{0:T(256)S(1)} %get-tuple-element.1018, s32[192]{0:T(256)S(1)} %dynamic_slice.87, s32[192]{0:T(256)S(1)} %dynamic_slice.88, s32[192]{0:T(256)S(1)} %get-tuple-element.1014), kind=kLoop, calls=%fused_computation.57.clone.1 | loop fusion | flops 147455 | bytes 39937 | tf_op jit(solution)/shard_map/while/body/eval_jaxpr/reduce_or | solution.py:152
  37.8 2.5 %conditional.8 = ((f32[1536,128]{1,0:T(8,128)S(1)}, f32[192,128]{1,0:T(8,128)S(1)}, f32[192,128]{1,0:T(8,128)S(1)})) conditional(s32[]{:T(128)} %convert_element_type.139, (f32[1536,128]{1,0:T(8,128)S(1)}, f32[192,128]{1,0:T(8,128)S(1)}, f32[192,128]{1,0:T(8,128)S(1)}) %tuple.108, (pred[192,192]{1,0:T(8,128)(4,1)S(1)}, ...), branch_computations={%region_13.13_spmd, %region_14.14_spmd} | conditional | flops 379797504 | bytes 10223648 | solution.py:152
  40.8 1.5 %collective-permute-start.3 = (bf16[192,128]{1,0:T(8,128)(2,1)S(1)}, bf16[192,128]{1,0:T(8,128)(2,1)S(1)}, u32[]{:S(2)}, u32[]{:S(2)}) collective-permute-start(bf16[192,128]{1,0:T(8,128)(2,1)S(1)} %convert_element_type.142), channel_id=1, source_target_pairs={{24,0},{0,8},{8,16},{16,24},{25,1},{1,9},{9,17},{17,25},{26,2},{2,... | collective-permute-start | bytes 147464 | tf_op jit(solution)/shard_map/while/body/eval_jaxpr/ppermute | solution.py:18
  42.8 1.2 %collective-permute-done.2 = bf16[192,128]{1,0:T(8,128)(2,1)S(1)} collective-permute-done((bf16[192,128]{1,0:T(8,128)(2,1)S(1)}, bf16[192,128]{1,0:T(8,128)(2,1)S(1)}, u32[]{:S(2)}, u32[]{:S(2)}) %collective-permute-start.2) | collective-permute-done | bytes 49184 | tf_op jit(solution)/shard_map/while/body/eval_jaxpr/ppermute | solution.py:18
  44.5 1.3 %collective-permute-done = bf16[192,128]{1,0:T(8,128)(2,1)S(1)} collective-permute-done((bf16[192,128]{1,0:T(8,128)(2,1)S(1)}, bf16[192,128]{1,0:T(8,128)(2,1)S(1)}, u32[]{:S(2)}, u32[]{:S(2)}) %collective-permute-start) | collective-permute-done | bytes 49184 | tf_op jit(solution)/shard_map/while/body/eval_jaxpr/ppermute | solution.py:18
  46.5 0.8 %fusion.54 = (pred[]{:T(512)}, pred[192,192]{1,0:T(8,128)(4,1)S(1)}) fusion(s32[192]{0:T(256)S(1)} %get-tuple-element.1018, s32[192]{0:T(256)S(1)} %dynamic_slice.87, s32[192]{0:T(256)S(1)} %dynamic_slice.88, s32[192]{0:T(256)S(1)} %get-tuple-element.1014), kind=kLoop, calls=%fused_computation.57.clone.1 | loop fusion | flops 147455 | bytes 39937 | tf_op jit(solution)/shard_map/while/body/eval_jaxpr/reduce_or | solution.py:152
  47.9 2.5 %conditional.8 = ((f32[1536,128]{1,0:T(8,128)S(1)}, f32[192,128]{1,0:T(8,128)S(1)}, f32[192,128]{1,0:T(8,128)S(1)})) conditional(s32[]{:T(128)} %convert_element_type.139, (f32[1536,128]{1,0:T(8,128)S(1)}, f32[192,128]{1,0:T(8,128)S(1)}, f32[192,128]{1,0:T(8,128)S(1)}) %tuple.108, (pred[192,192]{1,0:T(8,128)(4,1)S(1)}, ...), branch_computations={%region_13.13_spmd, %region_14.14_spmd} | conditional | flops 379797504 | bytes 10223648 | solution.py:152
  50.6 1.0 %collective-permute-start.3 = (bf16[192,128]{1,0:T(8,128)(2,1)S(1)}, bf16[192,128]{1,0:T(8,128)(2,1)S(1)}, u32[]{:S(2)}, u32[]{:S(2)}) collective-permute-start(bf16[192,128]{1,0:T(8,128)(2,1)S(1)} %convert_element_type.142), channel_id=1, source_target_pairs={{24,0},{0,8},{8,16},{16,24},{25,1},{1,9},{9,17},{17,25},{26,2},{2,... | collective-permute-start | bytes 147464 | tf_op jit(solution)/shard_map/while/body/eval_jaxpr/ppermute | solution.py:18
  51.7 1.1 %collective-permute-start.1 = (bf16[192,128]{1,0:T(8,128)(2,1)S(1)}, bf16[192,128]{1,0:T(8,128)(2,1)S(1)}, u32[]{:S(2)}, u32[]{:S(2)}) collective-permute-start(bf16[192,128]{1,0:T(8,128)(2,1)S(1)} %copy.50), channel_id=1, source_target_pairs={{24,0},{0,8},{8,16},{16,24},{25,1},{1,9},{9,17},{17,25},{26,2},{2,... | collective-permute-start | bytes 147464 | tf_op jit(solution)/shard_map/while/body/eval_jaxpr/ppermute | solution.py:18
  52.8 1.2 %collective-permute-done.2 = bf16[192,128]{1,0:T(8,128)(2,1)S(1)} collective-permute-done((bf16[192,128]{1,0:T(8,128)(2,1)S(1)}, bf16[192,128]{1,0:T(8,128)(2,1)S(1)}, u32[]{:S(2)}, u32[]{:S(2)}) %collective-permute-start.2) | collective-permute-done | bytes 49184 | tf_op jit(solution)/shard_map/while/body/eval_jaxpr/ppermute | solution.py:18
  57.2 2.5 %conditional.8 = ((f32[1536,128]{1,0:T(8,128)S(1)}, f32[192,128]{1,0:T(8,128)S(1)}, f32[192,128]{1,0:T(8,128)S(1)})) conditional(s32[]{:T(128)} %convert_element_type.139, (f32[1536,128]{1,0:T(8,128)S(1)}, f32[192,128]{1,0:T(8,128)S(1)}, f32[192,128]{1,0:T(8,128)S(1)}) %tuple.108, (pred[192,192]{1,0:T(8,128)(4,1)S(1)}, ...), branch_computations={%region_13.13_spmd, %region_14.14_spmd} | conditional | flops 379797504 | bytes 10223648 | solution.py:152
  59.9 1.2 %collective-permute-start.3 = (bf16[192,128]{1,0:T(8,128)(2,1)S(1)}, bf16[192,128]{1,0:T(8,128)(2,1)S(1)}, u32[]{:S(2)}, u32[]{:S(2)}) collective-permute-start(bf16[192,128]{1,0:T(8,128)(2,1)S(1)} %convert_element_type.142), channel_id=1, source_target_pairs={{24,0},{0,8},{8,16},{16,24},{25,1},{1,9},{9,17},{17,25},{26,2},{2,... | collective-permute-start | bytes 147464 | tf_op jit(solution)/shard_map/while/body/eval_jaxpr/ppermute | solution.py:18
  61.2 1.0 %collective-permute-start.1 = (bf16[192,128]{1,0:T(8,128)(2,1)S(1)}, bf16[192,128]{1,0:T(8,128)(2,1)S(1)}, u32[]{:S(2)}, u32[]{:S(2)}) collective-permute-start(bf16[192,128]{1,0:T(8,128)(2,1)S(1)} %copy.50), channel_id=1, source_target_pairs={{24,0},{0,8},{8,16},{16,24},{25,1},{1,9},{9,17},{17,25},{26,2},{2,... | collective-permute-start | bytes 147464 | tf_op jit(solution)/shard_map/while/body/eval_jaxpr/ppermute | solution.py:18
  62.1 1.2 %collective-permute-done.2 = bf16[192,128]{1,0:T(8,128)(2,1)S(1)} collective-permute-done((bf16[192,128]{1,0:T(8,128)(2,1)S(1)}, bf16[192,128]{1,0:T(8,128)(2,1)S(1)}, u32[]{:S(2)}, u32[]{:S(2)}) %collective-permute-start.2) | collective-permute-done | bytes 49184 | tf_op jit(solution)/shard_map/while/body/eval_jaxpr/ppermute | solution.py:18
  65.2 1.0 %collective-permute-start.4 = (bf16[192,128]{1,0:T(8,128)(2,1)S(1)}, bf16[192,128]{1,0:T(8,128)(2,1)S(1)}, u32[]{:S(2)}, u32[]{:S(2)}) collective-permute-start(bf16[192,128]{1,0:T(8,128)(2,1)S(1)} %convert_element_type.108), channel_id=1, source_target_pairs={{24,0},{0,8},{8,16},{16,24},{25,1},{1,9},{9,17},{17,25},{26,2},{2,... | collective-permute-start | bytes 147464 | tf_op jit(solution)/shard_map/ppermute | solution.py:18
  66.3 0.9 %reshape.123 = bf16[192,1024]{1,0:T(8,128)(2,1)} reshape(bf16[1536,128]{1,0:T(8,128)(2,1)S(1)} %divide_convert_fusion) | data formatting | bytes 786432 | tf_op jit(solution)/shard_map/reshape | solution.py:192
  67.2 0.9 %reshape.125 = bf16[192,1024]{1,0:T(8,128)(2,1)} reshape(bf16[1536,128]{1,0:T(8,128)(2,1)S(1)} %multiply_convert_fusion) | data formatting | bytes 786432 | tf_op jit(solution)/shard_map/reshape | solution.py:189
  (124 shorter events, 28.3 us)
Async XLA Ops:
  33.3 1.0 %copy-start = (bf16[192,1024]{1,0:T(8,128)(2,1)S(1)}, bf16[192,1024]{1,0:T(8,128)(2,1)}, u32[]{:S(2)}) copy-start(bf16[192,1024]{1,0:T(8,128)(2,1)} %param.19) | copy-start | bytes 1179652
  40.4 3.6 %collective-permute-start.2 = (bf16[192,128]{1,0:T(8,128)(2,1)S(1)}, bf16[192,128]{1,0:T(8,128)(2,1)S(1)}, u32[]{:S(2)}, u32[]{:S(2)}) collective-permute-start(bf16[192,128]{1,0:T(8,128)(2,1)S(1)} %convert_element_type.140), channel_id=1, source_target_pairs={{24,0},{0,8},{8,16},{16,24},{25,1},{1,9},{9,17},{17,25},{26,2},{2,... | collective-permute-start | bytes 147464 | tf_op jit(solution)/shard_map/while/body/eval_jaxpr/ppermute | solution.py:18
  40.8 3.7 %collective-permute-start.3 = (bf16[192,128]{1,0:T(8,128)(2,1)S(1)}, bf16[192,128]{1,0:T(8,128)(2,1)S(1)}, u32[]{:S(2)}, u32[]{:S(2)}) collective-permute-start(bf16[192,128]{1,0:T(8,128)(2,1)S(1)} %convert_element_type.142), channel_id=1, source_target_pairs={{24,0},{0,8},{8,16},{16,24},{25,1},{1,9},{9,17},{17,25},{26,2},{2,... | collective-permute-start | bytes 147464 | tf_op jit(solution)/shard_map/while/body/eval_jaxpr/ppermute | solution.py:18
  42.3 3.5 %collective-permute-start = (bf16[192,128]{1,0:T(8,128)(2,1)S(1)}, bf16[192,128]{1,0:T(8,128)(2,1)S(1)}, u32[]{:S(2)}, u32[]{:S(2)}) collective-permute-start(bf16[192,128]{1,0:T(8,128)(2,1)S(1)} %copy.49), channel_id=1, source_target_pairs={{24,0},{0,8},{8,16},{16,24},{25,1},{1,9},{9,17},{17,25},{26,2},{2,... | collective-permute-start | bytes 147464 | tf_op jit(solution)/shard_map/while/body/eval_jaxpr/ppermute | solution.py:18
  42.6 3.7 %collective-permute-start.1 = (bf16[192,128]{1,0:T(8,128)(2,1)S(1)}, bf16[192,128]{1,0:T(8,128)(2,1)S(1)}, u32[]{:S(2)}, u32[]{:S(2)}) collective-permute-start(bf16[192,128]{1,0:T(8,128)(2,1)S(1)} %copy.50), channel_id=1, source_target_pairs={{24,0},{0,8},{8,16},{16,24},{25,1},{1,9},{9,17},{17,25},{26,2},{2,... | collective-permute-start | bytes 147464 | tf_op jit(solution)/shard_map/while/body/eval_jaxpr/ppermute | solution.py:18
  50.5 3.6 %collective-permute-start.2 = (bf16[192,128]{1,0:T(8,128)(2,1)S(1)}, bf16[192,128]{1,0:T(8,128)(2,1)S(1)}, u32[]{:S(2)}, u32[]{:S(2)}) collective-permute-start(bf16[192,128]{1,0:T(8,128)(2,1)S(1)} %convert_element_type.140), channel_id=1, source_target_pairs={{24,0},{0,8},{8,16},{16,24},{25,1},{1,9},{9,17},{17,25},{26,2},{2,... | collective-permute-start | bytes 147464 | tf_op jit(solution)/shard_map/while/body/eval_jaxpr/ppermute | solution.py:18
  50.6 4.0 %collective-permute-start.3 = (bf16[192,128]{1,0:T(8,128)(2,1)S(1)}, bf16[192,128]{1,0:T(8,128)(2,1)S(1)}, u32[]{:S(2)}, u32[]{:S(2)}) collective-permute-start(bf16[192,128]{1,0:T(8,128)(2,1)S(1)} %convert_element_type.142), channel_id=1, source_target_pairs={{24,0},{0,8},{8,16},{16,24},{25,1},{1,9},{9,17},{17,25},{26,2},{2,... | collective-permute-start | bytes 147464 | tf_op jit(solution)/shard_map/while/body/eval_jaxpr/ppermute | solution.py:18
  51.6 3.5 %collective-permute-start = (bf16[192,128]{1,0:T(8,128)(2,1)S(1)}, bf16[192,128]{1,0:T(8,128)(2,1)S(1)}, u32[]{:S(2)}, u32[]{:S(2)}) collective-permute-start(bf16[192,128]{1,0:T(8,128)(2,1)S(1)} %copy.49), channel_id=1, source_target_pairs={{24,0},{0,8},{8,16},{16,24},{25,1},{1,9},{9,17},{17,25},{26,2},{2,... | collective-permute-start | bytes 147464 | tf_op jit(solution)/shard_map/while/body/eval_jaxpr/ppermute | solution.py:18
  51.7 4.0 %collective-permute-start.1 = (bf16[192,128]{1,0:T(8,128)(2,1)S(1)}, bf16[192,128]{1,0:T(8,128)(2,1)S(1)}, u32[]{:S(2)}, u32[]{:S(2)}) collective-permute-start(bf16[192,128]{1,0:T(8,128)(2,1)S(1)} %copy.50), channel_id=1, source_target_pairs={{24,0},{0,8},{8,16},{16,24},{25,1},{1,9},{9,17},{17,25},{26,2},{2,... | collective-permute-start | bytes 147464 | tf_op jit(solution)/shard_map/while/body/eval_jaxpr/ppermute | solution.py:18
  59.8 3.6 %collective-permute-start.2 = (bf16[192,128]{1,0:T(8,128)(2,1)S(1)}, bf16[192,128]{1,0:T(8,128)(2,1)S(1)}, u32[]{:S(2)}, u32[]{:S(2)}) collective-permute-start(bf16[192,128]{1,0:T(8,128)(2,1)S(1)} %convert_element_type.140), channel_id=1, source_target_pairs={{24,0},{0,8},{8,16},{16,24},{25,1},{1,9},{9,17},{17,25},{26,2},{2,... | collective-permute-start | bytes 147464 | tf_op jit(solution)/shard_map/while/body/eval_jaxpr/ppermute | solution.py:18
  59.9 4.0 %collective-permute-start.3 = (bf16[192,128]{1,0:T(8,128)(2,1)S(1)}, bf16[192,128]{1,0:T(8,128)(2,1)S(1)}, u32[]{:S(2)}, u32[]{:S(2)}) collective-permute-start(bf16[192,128]{1,0:T(8,128)(2,1)S(1)} %convert_element_type.142), channel_id=1, source_target_pairs={{24,0},{0,8},{8,16},{16,24},{25,1},{1,9},{9,17},{17,25},{26,2},{2,... | collective-permute-start | bytes 147464 | tf_op jit(solution)/shard_map/while/body/eval_jaxpr/ppermute | solution.py:18
  61.1 3.5 %collective-permute-start = (bf16[192,128]{1,0:T(8,128)(2,1)S(1)}, bf16[192,128]{1,0:T(8,128)(2,1)S(1)}, u32[]{:S(2)}, u32[]{:S(2)}) collective-permute-start(bf16[192,128]{1,0:T(8,128)(2,1)S(1)} %copy.49), channel_id=1, source_target_pairs={{24,0},{0,8},{8,16},{16,24},{25,1},{1,9},{9,17},{17,25},{26,2},{2,... | collective-permute-start | bytes 147464 | tf_op jit(solution)/shard_map/while/body/eval_jaxpr/ppermute | solution.py:18
  61.2 4.0 %collective-permute-start.1 = (bf16[192,128]{1,0:T(8,128)(2,1)S(1)}, bf16[192,128]{1,0:T(8,128)(2,1)S(1)}, u32[]{:S(2)}, u32[]{:S(2)}) collective-permute-start(bf16[192,128]{1,0:T(8,128)(2,1)S(1)} %copy.50), channel_id=1, source_target_pairs={{24,0},{0,8},{8,16},{16,24},{25,1},{1,9},{9,17},{17,25},{26,2},{2,... | collective-permute-start | bytes 147464 | tf_op jit(solution)/shard_map/while/body/eval_jaxpr/ppermute | solution.py:18
  65.1 3.7 %collective-permute-start.5 = (bf16[192,128]{1,0:T(8,128)(2,1)S(1)}, bf16[192,128]{1,0:T(8,128)(2,1)S(1)}, u32[]{:S(2)}, u32[]{:S(2)}) collective-permute-start(bf16[192,128]{1,0:T(8,128)(2,1)S(1)} %convert_element_type.111), channel_id=1, source_target_pairs={{24,0},{0,8},{8,16},{16,24},{25,1},{1,9},{9,17},{17,25},{26,2},{2,... | collective-permute-start | bytes 147464 | tf_op jit(solution)/shard_map/ppermute | solution.py:18
  65.2 4.2 %collective-permute-start.4 = (bf16[192,128]{1,0:T(8,128)(2,1)S(1)}, bf16[192,128]{1,0:T(8,128)(2,1)S(1)}, u32[]{:S(2)}, u32[]{:S(2)}) collective-permute-start(bf16[192,128]{1,0:T(8,128)(2,1)S(1)} %convert_element_type.108), channel_id=1, source_target_pairs={{24,0},{0,8},{8,16},{16,24},{25,1},{1,9},{9,17},{17,25},{26,2},{2,... | collective-permute-start | bytes 147464 | tf_op jit(solution)/shard_map/ppermute | solution.py:18
where the time goes:
time: 72 us; the launch traced here: 70.6 us
  local copies, waits for them, and re-layouts  13 us (18%)
  blocking collectives  12.4 us (17%)
  waiting for transfers between devices  10.6 us (15%)
  other arithmetic  9.51 us (13%)
  matrix products  9.19 us (13%)
  starting transfers between devices  8 us (11%)
  loops' own time  6.57 us (9%)
  between operations  1.39 us (2%)
    ppermute x14, waiting for transfers between devices, from_behind(): return lax.ppermute(block, axis, route)  10.6 us
    ppermute x14, starting transfers between devices, from_behind(): return lax.ppermute(block, axis, route)  8 us
    all_gather x1, blocking collectives, local(): lax.all_gather(value_vectors, 'ctx', axis=0, tiled=True)  6.87 us
    all_gather x1, blocking collectives, local(): lax.all_gather(key_vectors, 'ctx', axis=0, tiled=True)  5.58 us
    another operation x1, loops' own time, over_blocks(): lax.scan(advance, running, (stacked, jnp.arange(row_count // block_keys,...  4 us
    reduce_or x4, other arithmetic, update(): return lax.cond(jnp.any(allowed), update_active, unchanged, running)  3.02 us
    unnamed x5, local copies, waits for them, and re-layouts  2.91 us
    dot_general x6, matrix products, logits(): lax.dot_general(query_flat, key_rows, (((1,), (1,)), ((), ())), preferred...  2.57 us
  transfers between devices with their start and end apart: 14, of which 14 were waited for; matrix products, arithmetic and copies ran while one was open for 3% of the time, Pallas kernels for 0%

commit v1 on v0

v1 whole, which is shorter than its diff:
```python
import math

import jax
import jax.numpy as jnp
from jax import lax
from jax.experimental import pallas as pl
from jax.experimental.pallas import tpu as pltpu
from jax.sharding import PartitionSpec as P

DH = 128
TILE = 384
FILL = -1e30

NT = (((1,), (1,)), ((), ()))
NN = (((1,), (0,)), ((), ()))
TN = (((0,), (0,)), ((), ()))


def mm(a, b, dims):
    return lax.dot_general(a, b, dims, preferred_element_type=jnp.float32)


def attention_kernel(n, heads, span, spans_all, docs, so, dl, own_ref, *refs):
    spans_own = spans_all // n
    tok = span * spans_own
    rows = heads * span
    scale = 1.0 / math.sqrt(DH)
    grow = scale * math.log2(math.e)
    q_ref, g_ref = refs[0], refs[1]
    kv = refs[2 : 2 + n]
    outs = refs[2 + n :]
    att_ref, dq_ref = outs[0], outs[1]
    parts = outs[2 : 2 + n]
    ks, vs, dk, dv, qs, gs, bias, sc, dp, pb, db, mx, ls, dd, oa, qa = outs[2 + n :]
    pad = TILE
    own = own_ref[0]

    def place(slot):
        return pl.multiple_of(so[slot] * span + pad, 16)

    ks[0:pad, :] = jnp.zeros((pad, DH), ks.dtype)
    vs[0:pad, :] = jnp.zeros((pad, DH), vs.dtype)
    dk[...] = jnp.zeros(dk.shape, dk.dtype)
    dv[...] = jnp.zeros(dv.shape, dv.dtype)
    for m in range(n):
        base = (own ^ m) * spans_own
        for j in range(spans_own):
            at = place(base + j)
            ks[pl.ds(at, span), :] = kv[m][j * span : (j + 1) * span, 0:DH]
            vs[pl.ds(at, span), :] = kv[m][j * span : (j + 1) * span, DH : 2 * DH]

    for j in range(spans_own):
        first = so[own * spans_own + j] * span
        stop = first + span
        edge = jnp.int32(0)
        begin = jnp.int32(0)
        pos = first + lax.broadcasted_iota(jnp.int32, (span, TILE), 0)
        begin_row = jnp.zeros((span, TILE), jnp.int32)
        for d in range(docs):
            edge = edge + dl[d]
            begin = jnp.where(edge <= first, edge, begin)
            begin_row = jnp.where(edge <= pos, edge, begin_row)
        count = (stop - begin + TILE - 1) // TILE
        lane = lax.broadcasted_iota(jnp.int32, (span, TILE), 1)
        for h in range(heads):
            at = slice(h * span, (h + 1) * span)
            qs[at, :] = q_ref[j * span : (j + 1) * span, h * DH : (h + 1) * DH]
            gs[at, :] = g_ref[j * span : (j + 1) * span, h * DH : (h + 1) * DH]

        def tile_at(t):
            return pl.multiple_of(stop + pad - (t + 1) * TILE, 16)

        def bias_of(t):
            key_pos = lane + (stop - (t + 1) * TILE)
            return jnp.where((key_pos <= pos) & (key_pos >= begin_row), 0.0, FILL)

        def finish(t, h, e, grads, inv, mean):
            at = slice(h * span, (h + 1) * span)
            p = e * inv
            pb[at, :] = p.astype(jnp.bfloat16)
            db[at, :] = (p * (grads - mean)).astype(jnp.bfloat16)

        def products(t):
            start = tile_at(t)
            kt = ks[pl.ds(start, TILE), :]
            vt = vs[pl.ds(start, TILE), :]
            p = pb[...]
            d = db[...]
            dv[pl.ds(start, TILE), :] += mm(p, gs[...], TN)
            dk[pl.ds(start, TILE), :] += mm(d, qs[...], TN)
            return mm(p, vt, NN), mm(d, kt, NN)

        def store(o, dq):
            for h in range(heads):
                at = slice(h * span, (h + 1) * span)
                to = (slice(j * span, (j + 1) * span), slice(h * DH, (h + 1) * DH))
                att_ref[to] = o[at, :].astype(att_ref.dtype)
                dq_ref[to] = (dq[at, :] * scale).astype(dq_ref.dtype)

        @pl.when(count == 1)
        def _():
            start = tile_at(0)
            kt = ks[pl.ds(start, TILE), :]
            vt = vs[pl.ds(start, TILE), :]
            bias[...] = bias_of(0)
            sc[0] = mm(qs[...], kt, NT)
            dp[0] = mm(gs[...], vt, NT)
            for h in range(heads):
                at = slice(h * span, (h + 1) * span)
                s = sc[0, at, :] + bias[...]
                e = jnp.exp2((s - jnp.max(s, axis=1, keepdims=True)) * grow)
                grads = dp[0, at, :]
                inv = 1.0 / jnp.sum(e, axis=1, keepdims=True)
                mean = jnp.sum(e * grads, axis=1, keepdims=True) * inv
                finish(0, h, e, grads, inv, mean)
            store(*products(0))

        @pl.when(count > 1)
        def _():
            mx[...] = jnp.full(mx.shape, FILL, mx.dtype)
            ls[...] = jnp.zeros(ls.shape, ls.dtype)
            dd[...] = jnp.zeros(dd.shape, dd.dtype)
            oa[...] = jnp.zeros(oa.shape, oa.dtype)
            qa[...] = jnp.zeros(qa.shape, qa.dtype)

            def first_pass(t, c):
                start = tile_at(t)
                bias[...] = bias_of(t)
                s_all = mm(qs[...], ks[pl.ds(start, TILE), :], NT)
                dp[t] = mm(gs[...], vs[pl.ds(start, TILE), :], NT)
                for h in range(heads):
                    at = slice(h * span, (h + 1) * span)
                    s = s_all[at, :] + bias[...]
                    sc[t, at, :] = s
                    mx[at, :] = jnp.maximum(mx[at, :], jnp.max(s, axis=1, keepdims=True))
                return c

            def second_pass(t, c):
                for h in range(heads):
                    at = slice(h * span, (h + 1) * span)
                    e = jnp.exp2((sc[t, at, :] - mx[at, 0:1]) * grow)
                    sc[t, at, :] = e
                    ls[at, :] += jnp.sum(e, axis=1, keepdims=True)
                    dd[at, :] += jnp.sum(e * dp[t, at, :], axis=1, keepdims=True)
                return c

            def third_pass(t, c):
                for h in range(heads):
                    at = slice(h * span, (h + 1) * span)
                    inv = 1.0 / ls[at, 0:1]
                    finish(t, h, sc[t, at, :], dp[t, at, :], inv, dd[at, 0:1] * inv)
                o, dq = products(t)
                oa[...] += o
                qa[...] += dq
                return c

            lax.fori_loop(0, count, first_pass, 0)
            lax.fori_loop(0, count, second_pass, 0)
            lax.fori_loop(0, count, third_pass, 0)
            store(oa[...], qa[...])

    for m in range(n):
        base = (own ^ m) * spans_own
        for j in range(spans_own):
            at = place(base + j)
            to = slice(j * span, (j + 1) * span)
            parts[m][to, 0:DH] = (dk[pl.ds(at, span), :] * scale).astype(parts[m].dtype)
            parts[m][to, DH : 2 * DH] = dv[pl.ds(at, span), :].astype(parts[m].dtype)


def local(queries, key_vectors, value_vectors, out_grad, span_order, doc_lengths):
    tok, width = queries.shape
    n = lax.axis_size("ctx")
    heads = width // DH
    spans_all = span_order.shape[0]
    docs = doc_lengths.shape[0]
    seq = tok * n
    span = seq // spans_all
    rows = heads * span
    tiles = -(-seq // TILE)
    own = lax.axis_index("ctx").astype(jnp.int32).reshape(1)

    def swap(x, m):
        return lax.ppermute(x, "ctx", [(i, i ^ m) for i in range(n)])

    both = jnp.concatenate([key_vectors, value_vectors], axis=1)
    kv = [both] + [swap(both, m) for m in range(1, n)]

    vm = pl.BlockSpec(memory_space=pltpu.VMEM)
    sm = pl.BlockSpec(memory_space=pltpu.SMEM)
    bf, f32 = jnp.bfloat16, jnp.float32
    out_shape = [
        jax.ShapeDtypeStruct((tok, width), bf),
        jax.ShapeDtypeStruct((tok, width), bf),
        jax.ShapeDtypeStruct((tok, 2 * DH), f32),
    ] + [jax.ShapeDtypeStruct((tok, 2 * DH), bf)] * (n - 1)
    V = pltpu.VMEM
    scratch = [
        V((TILE + seq, DH), bf),
        V((TILE + seq, DH), bf),
        V((TILE + seq, DH), f32),
        V((TILE + seq, DH), f32),
        V((rows, DH), bf),
        V((rows, DH), bf),
        V((span, TILE), f32),
        V((tiles, rows, TILE), f32),
        V((tiles, rows, TILE), f32),
        V((rows, TILE), bf),
        V((rows, TILE), bf),
        V((rows, DH), f32),
        V((rows, DH), f32),
        V((rows, DH), f32),
        V((rows, DH), f32),
        V((rows, DH), f32),
    ]

    def body(*refs):
        attention_kernel(n, heads, span, spans_all, docs, *refs)

    res = pl.pallas_call(
        body,
        out_shape=out_shape,
        in_specs=[sm, sm, sm] + [vm] * (2 + n),
        out_specs=[vm] * len(out_shape),
        scratch_shapes=scratch,
        compiler_params=pltpu.CompilerParams(vmem_limit_bytes=(16 + 3 * tiles) << 20),
        name="attention",
    )(span_order, doc_lengths, own, queries, out_grad, *kv)
    got = [swap(res[2 + m], m) for m in range(1, n)]

    def merge(own_ref, *refs):
        total = own_ref[...]
        for ref in refs[:-2]:
            total = total + ref[...].astype(f32)
        refs[-2][...] = total[:, :DH].astype(bf)
        refs[-1][...] = total[:, DH:].astype(bf)

    half = jax.ShapeDtypeStruct((tok, DH), bf)
    key_grad, value_grad = pl.pallas_call(
        merge,
        out_shape=[half, half],
        in_specs=[vm] * n,
        out_specs=[vm, vm],
        compiler_params=pltpu.CompilerParams(vmem_limit_bytes=4 << 20),
        name="merge",
    )(res[2], *got)
    return res[0], res[1], key_grad, value_grad


def solution(mesh):
    rows = P(("seq", "ctx"), None)
    return jax.shard_map(
        local,
        mesh=mesh,
        in_specs=(rows, rows, rows, rows, P("seq"), P("seq")),
        out_specs=(rows, rows, rows, rows),
        check_vma=False,
    )
```

time: 72 us -> 24.9 us (0.35); the launches traced: 70.6 us -> 24.6 us
  blocking collectives: 12.4 us -> 0 us
  local copies, waits for them, and re-layouts: 13 us -> 2.84 us
  other arithmetic: 9.51 us -> 0 us
  matrix products: 9.19 us -> 0 us
  loops' own time: 6.57 us -> 0 us
  Pallas kernels: 0 us -> 5.62 us
  starting transfers between devices: 8 us -> 5.57 us
    all_gather x2 -> x0, blocking collectives: 12.4 us -> none  [the longest x1 6.87 us: local(): lax.all_gather(value_vectors, 'ctx', axis=0, tiled=True)]
    dot_general x21 -> x0, matrix products: 9.19 us -> none  [the longest x6 2.57 us: logits(): lax.dot_general(query_flat, key_rows, (((1,), (1,)), ((), ())), preferred...]
    another operation x9 -> x0, loops' own time: 6.57 us -> none  [the longest x1 4 us: over_blocks(): lax.scan(advance, running, (stacked, jnp.arange(row_count // block_keys,...]
    pallas_call x0 -> x2, Pallas kernels: none -> 5.62 us  [the longest x1 4.94 us: local(): pl.pallas_call(body, out_shape=out_shape, in_specs=[sm, sm, sm] + [vm] *...]
    reduce_or x7 -> x0, other arithmetic: 5.28 us -> none  [the longest x4 3.02 us: update(): return lax.cond(jnp.any(allowed), update_active, unchanged, running)]
    broadcast_in_dim x14 -> x0, local copies, waits for them, and re-layouts: 3.93 us -> none  [the longest x6 1.99 us: forward_active(): scores = jnp.where(mask_wide, logits(key_rows), negative_fill)]
    reshape x4 -> x0, local copies, waits for them, and re-layouts: 3.16 us -> none  [the longest x1 1.16 us: local(): query_flat = queries.reshape(tok_rows * HQ, DH)]
    dynamic_slice x16 -> x0, local copies, waits for them, and re-layouts: 2.74 us -> none  [the longest x3 1.76 us: over_blocks(): lax.scan(advance, running, (stacked, jnp.arange(row_count // block_keys,...]
  transfers between devices with their start and end apart: 14 -> 6, of which waited for: 14 -> 4; matrix products, arithmetic and copies ran while one was open for 3% -> 0% of each run, Pallas kernels for 0% -> 0%
where the time goes in v1:
time: 24.9 us; the launch traced here: 24.6 us
  waiting for transfers between devices  9.94 us (40%)
  Pallas kernels  5.62 us (23%)
  starting transfers between devices  5.57 us (22%)
  local copies, waits for them, and re-layouts  2.84 us (11%)
  between operations  0.68 us (3%)
    ppermute x6, waiting for transfers between devices, swap(): return lax.ppermute(x, 'ctx', [(i, i ^ m) for i in range(n)])  9.94 us
    ppermute x6, starting transfers between devices, swap(): return lax.ppermute(x, 'ctx', [(i, i ^ m) for i in range(n)])  5.57 us
    pallas_call x1, Pallas kernels, local(): pl.pallas_call(body, out_shape=out_shape, in_specs=[sm, sm, sm] + [vm] *...  4.94 us
    unnamed x11, local copies, waits for them, and re-layouts  2.82 us
    pallas_call x1, Pallas kernels, local(): pl.pallas_call(merge, out_shape=[half, half], in_specs=[vm] * n, out_spec...  0.68 us
  transfers between devices with their start and end apart: 6, of which 4 were waited for; matrix products, arithmetic and copies ran while one was open for 0% of the time, Pallas kernels for 0%

profile of v1, /device:TPU:0, one launch (start us, length us, event | category | flops | bytes accessed | tf_op | source)
XLA Modules:
  0.0 24.6 jit_solution(277981689826567668)
XLA Ops:
  0.6 0.0 copy-start.4
  0.6 0.8 %constant_dynamic-update-slice_fusion.1 = bf16[192,256]{1,0:T(8,128)(2,1)S(1)} fusion(bf16[192,128]{1,0:T(8,128)(2,1)} %param.7), kind=kLoop, calls=%fused_computation.1 | loop fusion | bytes 98304
  1.5 0.0 copy-done.4
  1.5 2.5 %collective-permute-start.2 = (bf16[192,256]{1,0:T(8,128)(2,1)S(1)}, bf16[192,256]{1,0:T(8,128)(2,1)S(1)}, u32[]{:S(2)}, u32[]{:S(2)}) collective-permute-start(bf16[192,256]{1,0:T(8,128)(2,1)S(1)} %constant_dynamic-update-slice_fusion.refs_5_), channel_id=1, source_target_pairs={{0,24},{8,16},{16,8},{24,0},{1,25},{9,17},{17,9},{25,1},{2,26},{10... | collective-permute-start | bytes 294920 | tf_op jit(solution)/shard_map/ppermute | solution.py:184
  4.0 0.6 %collective-permute-start.1 = (bf16[192,256]{1,0:T(8,128)(2,1)S(1)}, bf16[192,256]{1,0:T(8,128)(2,1)S(1)}, u32[]{:S(2)}, u32[]{:S(2)}) collective-permute-start(bf16[192,256]{1,0:T(8,128)(2,1)S(1)} %constant_dynamic-update-slice_fusion.refs_5_), channel_id=1, source_target_pairs={{0,16},{8,24},{16,0},{24,8},{1,17},{9,25},{17,1},{25,9},{2,18},{10... | collective-permute-start | bytes 294920 | tf_op jit(solution)/shard_map/ppermute | solution.py:184
  4.6 0.0 collective-permute-start
  4.6 0.0 copy-start.2
  4.7 0.0 copy-start.3
  4.7 2.5 %collective-permute-done.2.refs_8_ = bf16[192,256]{1,0:T(8,128)(2,1)S(1)} collective-permute-done((bf16[192,256]{1,0:T(8,128)(2,1)S(1)}, bf16[192,256]{1,0:T(8,128)(2,1)S(1)}, u32[]{:S(2)}, u32[]{:S(2)}) %collective-permute-start.2) | collective-permute-done | bytes 98336 | tf_op jit(solution)/shard_map/ppermute | solution.py:184
  7.2 2.3 %collective-permute-done.1.refs_7_ = bf16[192,256]{1,0:T(8,128)(2,1)S(1)} collective-permute-done((bf16[192,256]{1,0:T(8,128)(2,1)S(1)}, bf16[192,256]{1,0:T(8,128)(2,1)S(1)}, u32[]{:S(2)}, u32[]{:S(2)}) %collective-permute-start.1) | collective-permute-done | bytes 98336 | tf_op jit(solution)/shard_map/ppermute | solution.py:184
  9.4 0.0 collective-permute-done.refs_6_
  9.4 0.0 copy-done.2
  9.4 0.0 copy-done.3
  9.4 0.0 copy-start
  9.5 1.0 %copy-done = bf16[192,1024]{1,0:T(8,128)(2,1)S(1)} copy-done((bf16[192,1024]{1,0:T(8,128)(2,1)S(1)}, bf16[192,1024]{1,0:T(8,128)(2,1)}, u32[]{:S(2)}) %copy-start) | copy-done | bytes 393240
  10.4 0.0 copy-start.1
  10.4 1.0 %copy-done.1 = bf16[192,1024]{1,0:T(8,128)(2,1)S(1)} copy-done((bf16[192,1024]{1,0:T(8,128)(2,1)S(1)}, bf16[192,1024]{1,0:T(8,128)(2,1)}, u32[]{:S(2)}) %copy-start.1) | copy-done | bytes 393240
  11.4 4.9 %attention.1 = (bf16[192,1024]{1,0:T(8,128)(2,1)}, bf16[192,1024]{1,0:T(8,128)(2,1)}, f32[192,256]{1,0:T(8,128)S(1)}, bf16[192,256]{1,0:T(8,128)(2,1)S(1)}, bf16...) custom-call(s32[8]{0:T(128)S(1)} %copy-done.2, s32[6]{0:T(128)S(1)} %copy-done.3, s32[1]{0:T(128)} %bitcast.refs_2_, ...), custom_call_target="tpu_custom_call" | custom-call | tf_op jit(solution)/shard_map/attention/pallas_call | solution.py:220
  16.4 0.0 collective-permute-start.3
  16.4 2.4 %collective-permute-start.4 = (bf16[192,256]{1,0:T(8,128)(2,1)S(1)}, bf16[192,256]{1,0:T(8,128)(2,1)S(1)}, u32[]{:S(2)}, u32[]{:S(2)}) collective-permute-start(bf16[192,256]{1,0:T(8,128)(2,1)S(1)} %get-tuple-element.16), channel_id=1, source_target_pairs={{0,16},{8,24},{16,0},{24,8},{1,17},{9,25},{17,1},{25,9},{2,18},{10... | collective-permute-start | bytes 294920 | tf_op jit(solution)/shard_map/ppermute | solution.py:184
  18.8 0.0 collective-permute-start.5
  18.8 0.0 collective-permute-done.3.refs_0_
  18.8 3.6 %collective-permute-done.4.refs_1_ = bf16[192,256]{1,0:T(8,128)(2,1)S(1)} collective-permute-done((bf16[192,256]{1,0:T(8,128)(2,1)S(1)}, bf16[192,256]{1,0:T(8,128)(2,1)S(1)}, u32[]{:S(2)}, u32[]{:S(2)}) %collective-permute-start.4) | collective-permute-done | bytes 98336 | tf_op jit(solution)/shard_map/ppermute | solution.py:184
  22.4 1.5 %collective-permute-done.5.refs_2_ = bf16[192,256]{1,0:T(8,128)(2,1)S(1)} collective-permute-done((bf16[192,256]{1,0:T(8,128)(2,1)S(1)}, bf16[192,256]{1,0:T(8,128)(2,1)S(1)}, u32[]{:S(2)}, u32[]{:S(2)}) %collective-permute-start.5) | collective-permute-done | bytes 98336 | tf_op jit(solution)/shard_map/ppermute | solution.py:184
  24.0 0.7 %merge.1 = (bf16[192,128]{1,0:T(8,128)(2,1)}, bf16[192,128]{1,0:T(8,128)(2,1)}) custom-call(f32[192,256]{1,0:T(8,128)S(1)} %get-tuple-element.14.own_ref, bf16[192,256]{1,0:T(8,128)(2,1)S(1)} %collective-permute-done.3.refs_0_, bf16[192,256]{1,0:T(8,128)(2,1)S(1)} %collective-permute-done.4.refs_1_, bf16[192,256]{1,0:T(8,128)(2,1)S(1)} %collective-permute-done.5.refs_2_), custom_call_target="tpu_custom_call" | custom-call | tf_op jit(solution)/shard_map/merge/pallas_call | solution.py:239
  (1 shorter events, 0.0 us)
Async XLA Ops:
  0.6 0.8 %copy-start.4 = (bf16[192,128]{1,0:T(8,128)(2,1)S(1)}, bf16[192,128]{1,0:T(8,128)(2,1)}, u32[]{:S(2)}) copy-start(bf16[192,128]{1,0:T(8,128)(2,1)} %param.8) | copy-start | bytes 147460
  1.5 5.7 %collective-permute-start.2 = (bf16[192,256]{1,0:T(8,128)(2,1)S(1)}, bf16[192,256]{1,0:T(8,128)(2,1)S(1)}, u32[]{:S(2)}, u32[]{:S(2)}) collective-permute-start(bf16[192,256]{1,0:T(8,128)(2,1)S(1)} %constant_dynamic-update-slice_fusion.refs_5_), channel_id=1, source_target_pairs={{0,24},{8,16},{16,8},{24,0},{1,25},{9,17},{17,9},{25,1},{2,26},{10... | collective-permute-start | bytes 294920 | tf_op jit(solution)/shard_map/ppermute | solution.py:184
  4.0 5.5 %collective-permute-start.1 = (bf16[192,256]{1,0:T(8,128)(2,1)S(1)}, bf16[192,256]{1,0:T(8,128)(2,1)S(1)}, u32[]{:S(2)}, u32[]{:S(2)}) collective-permute-start(bf16[192,256]{1,0:T(8,128)(2,1)S(1)} %constant_dynamic-update-slice_fusion.refs_5_), channel_id=1, source_target_pairs={{0,16},{8,24},{16,0},{24,8},{1,17},{9,25},{17,1},{25,9},{2,18},{10... | collective-permute-start | bytes 294920 | tf_op jit(solution)/shard_map/ppermute | solution.py:184
  4.6 4.8 %collective-permute-start = (bf16[192,256]{1,0:T(8,128)(2,1)S(1)}, bf16[192,256]{1,0:T(8,128)(2,1)S(1)}, u32[]{:S(2)}, u32[]{:S(2)}) collective-permute-start(bf16[192,256]{1,0:T(8,128)(2,1)S(1)} %constant_dynamic-update-slice_fusion.refs_5_), channel_id=1, source_target_pairs={{0,8},{8,0},{16,24},{24,16},{1,9},{9,1},{17,25},{25,17},{2,10},{10... | collective-permute-start | bytes 294920 | tf_op jit(solution)/shard_map/ppermute | solution.py:184
  4.6 4.8 %copy-start.2 = (s32[8]{0:T(128)S(1)}, s32[8]{0:T(128)}, u32[]{:S(2)}) copy-start(s32[8]{0:T(128)} %refs_0_.1) | copy-start | bytes 100
  4.7 4.8 %copy-start.3 = (s32[6]{0:T(128)S(1)}, s32[6]{0:T(128)}, u32[]{:S(2)}) copy-start(s32[6]{0:T(128)} %refs_1_.1) | copy-start | bytes 76
  9.4 1.0 %copy-start = (bf16[192,1024]{1,0:T(8,128)(2,1)S(1)}, bf16[192,1024]{1,0:T(8,128)(2,1)}, u32[]{:S(2)}) copy-start(bf16[192,1024]{1,0:T(8,128)(2,1)} %refs_3_.1) | copy-start | bytes 1179652
  10.4 1.0 %copy-start.1 = (bf16[192,1024]{1,0:T(8,128)(2,1)S(1)}, bf16[192,1024]{1,0:T(8,128)(2,1)}, u32[]{:S(2)}) copy-start(bf16[192,1024]{1,0:T(8,128)(2,1)} %refs_4_.1) | copy-start | bytes 1179652
  16.4 2.4 %collective-permute-start.3 = (bf16[192,256]{1,0:T(8,128)(2,1)S(1)}, bf16[192,256]{1,0:T(8,128)(2,1)S(1)}, u32[]{:S(2)}, u32[]{:S(2)}) collective-permute-start(bf16[192,256]{1,0:T(8,128)(2,1)S(1)} %get-tuple-element.15), channel_id=1, source_target_pairs={{0,8},{8,0},{16,24},{24,16},{1,9},{9,1},{17,25},{25,17},{2,10},{10... | collective-permute-start | bytes 294920 | tf_op jit(solution)/shard_map/ppermute | solution.py:184
  16.4 6.0 %collective-permute-start.4 = (bf16[192,256]{1,0:T(8,128)(2,1)S(1)}, bf16[192,256]{1,0:T(8,128)(2,1)S(1)}, u32[]{:S(2)}, u32[]{:S(2)}) collective-permute-start(bf16[192,256]{1,0:T(8,128)(2,1)S(1)} %get-tuple-element.16), channel_id=1, source_target_pairs={{0,16},{8,24},{16,0},{24,8},{1,17},{9,25},{17,1},{25,9},{2,18},{10... | collective-permute-start | bytes 294920 | tf_op jit(solution)/shard_map/ppermute | solution.py:184
  18.8 5.2 %collective-permute-start.5 = (bf16[192,256]{1,0:T(8,128)(2,1)S(1)}, bf16[192,256]{1,0:T(8,128)(2,1)S(1)}, u32[]{:S(2)}, u32[]{:S(2)}) collective-permute-start(bf16[192,256]{1,0:T(8,128)(2,1)S(1)} %get-tuple-element.17), channel_id=1, source_target_pairs={{0,24},{8,16},{16,8},{24,0},{1,25},{9,17},{17,9},{25,1},{2,26},{10... | collective-permute-start | bytes 294920 | tf_op jit(solution)/shard_map/ppermute | solution.py:184

commit v2 on v1

v2 whole, which is shorter than its diff:
```python
import math

import jax
import jax.numpy as jnp
from jax import lax
from jax.experimental import pallas as pl
from jax.experimental.pallas import tpu as pltpu
from jax.sharding import PartitionSpec as P

DH = 128
TILE = 384
FILL = -1e30
SCALE = 1.0 / math.sqrt(DH)
GROW = SCALE * math.log2(math.e)

NT = (((1,), (1,)), ((), ()))
NN = (((1,), (0,)), ((), ()))
TN = (((0,), (0,)), ((), ()))


def mm(a, b, dims):
    return lax.dot_general(a, b, dims, preferred_element_type=jnp.float32)


def window(so, dl, slot, span, docs):
    first = so[slot] * span
    stop = first + span
    edge = jnp.int32(0)
    begin = jnp.int32(0)
    for d in range(docs):
        edge = edge + dl[d]
        begin = jnp.where(edge <= first, edge, begin)
    return first, stop, (stop - begin + TILE - 1) // TILE


def plan(meta, n, span, spans_all, docs):
    own = lax.axis_index("ctx")
    spans_own = spans_all // n
    dl = [meta[spans_all + d] for d in range(docs)]
    wins = [window(meta, dl, own * spans_own + j, span, docs) for j in range(spans_own)]
    short = wins[0][2] == 1
    for w in wins[1:]:
        short = short & (w[2] == 1)
    return own, dl, wins, short


def prepare_kernel(n, heads, span, spans_all, docs, meta, both, qs, gs, bias):
    own, dl, wins, short = plan(meta, n, span, spans_all, docs)
    tok = len(wins) * span
    for j, (first, stop, count) in enumerate(wins):
        for h in range(heads):
            to = slice(h * span, (h + 1) * span)
            cols = slice(h * DH, (h + 1) * DH)
            qs[j, to, :] = both[j * span : (j + 1) * span, cols]
            gs[j, to, :] = both[tok + j * span : tok + (j + 1) * span, cols]
        bias[j] = bias_tile(dl, docs, span, first, stop)


def bias_tile(dl, docs, span, first, tile_stop):
    pos = first + lax.broadcasted_iota(jnp.int32, (span, TILE), 0)
    edge = jnp.int32(0)
    begin_row = jnp.zeros((span, TILE), jnp.int32)
    for d in range(docs):
        edge = edge + dl[d]
        begin_row = jnp.where(edge <= pos, edge, begin_row)
    key_pos = lax.broadcasted_iota(jnp.int32, (span, TILE), 1) + (tile_stop - TILE)
    return jnp.where((key_pos <= pos) & (key_pos >= begin_row), 0.0, FILL)


def front_kernel(n, heads, span, spans_all, docs, meta, qs, gs, bias, *refs):
    own, dl, wins, short = plan(meta, n, span, spans_all, docs)
    spans_own = spans_all // n
    kv = refs[0:n]
    parts = refs[n : 2 * n]
    pb, db, kw, vw, oa, qa = refs[2 * n : 2 * n + 6]
    ks, vs, dk, dv, sc, dp, mx, ls, dd, more = refs[2 * n + 6 :]
    pad = TILE
    head_rows = [slice(h * span, (h + 1) * span) for h in range(heads)]
    ks[0:pad, :] = jnp.zeros((pad, DH), ks.dtype)
    vs[0:pad, :] = jnp.zeros((pad, DH), vs.dtype)
    dk[...] = jnp.zeros(dk.shape, dk.dtype)
    dv[...] = jnp.zeros(dv.shape, dv.dtype)

    def place(m, j):
        return pl.multiple_of(meta[(own ^ m) * spans_own + j] * span + pad, 16)

    for m in range(n):
        for j in range(spans_own):
            at = place(m, j)
            ks[pl.ds(at, span), :] = kv[m][j * span : (j + 1) * span, 0:DH]
            vs[pl.ds(at, span), :] = kv[m][j * span : (j + 1) * span, DH : 2 * DH]

    def tile_at(j, t):
        return pl.multiple_of(wins[j][1] + pad - (t + 1) * TILE, 16)

    def finish(j, h, e, grads, inv, mean):
        p = e * inv
        pb[j, head_rows[h], :] = p.astype(jnp.bfloat16)
        db[j, head_rows[h], :] = (p * (grads - mean)).astype(jnp.bfloat16)

    def key_side(j, t):
        start = tile_at(j, t)
        dv[pl.ds(start, TILE), :] += mm(pb[j], gs[j], TN)
        dk[pl.ds(start, TILE), :] += mm(db[j], qs[j], TN)

    @pl.when(short)
    def _():
        for j in range(spans_own):
            start = tile_at(j, 0)
            kw[j] = ks[pl.ds(start, TILE), :]
            vw[j] = vs[pl.ds(start, TILE), :]
        for j in range(spans_own):
            sc[j] = mm(qs[j], kw[j], NT)
            dp[j] = mm(gs[j], vw[j], NT)
            for h in range(heads):
                s = sc[j, head_rows[h], :] + bias[j]
                e = jnp.exp2((s - jnp.max(s, axis=1, keepdims=True)) * GROW)
                grads = dp[j, head_rows[h], :]
                inv = 1.0 / jnp.sum(e, axis=1, keepdims=True)
                mean = jnp.sum(e * grads, axis=1, keepdims=True) * inv
                finish(j, h, e, grads, inv, mean)
        for j in range(spans_own):
            key_side(j, 0)

    @pl.when(jnp.logical_not(short))
    def _():
        for j in range(spans_own):
            mx[...] = jnp.full(mx.shape, FILL, mx.dtype)
            ls[...] = jnp.zeros(ls.shape, ls.dtype)
            dd[...] = jnp.zeros(dd.shape, dd.dtype)
            oa[j] = jnp.zeros(oa.shape[1:], oa.dtype)
            qa[j] = jnp.zeros(qa.shape[1:], qa.dtype)

            def first_pass(t, c):
                start = tile_at(j, t)
                more[...] = bias_tile(dl, docs, span, wins[j][0], wins[j][1] - t * TILE)
                dp[t] = mm(qs[j], ks[pl.ds(start, TILE), :], NT)
                for at in head_rows:
                    s = dp[t, at, :] + more[...]
                    sc[t, at, :] = s
                    mx[at, :] = jnp.maximum(mx[at, :], jnp.max(s, axis=1, keepdims=True))
                dp[t] = mm(gs[j], vs[pl.ds(start, TILE), :], NT)
                return c

            def second_pass(t, c):
                for at in head_rows:
                    e = jnp.exp2((sc[t, at, :] - mx[at, 0:1]) * GROW)
                    sc[t, at, :] = e
                    ls[at, :] += jnp.sum(e, axis=1, keepdims=True)
                    dd[at, :] += jnp.sum(e * dp[t, at, :], axis=1, keepdims=True)
                return c

            def third_pass(t, c):
                start = tile_at(j, t)
                for h in range(heads):
                    at = head_rows[h]
                    inv = 1.0 / ls[at, 0:1]
                    finish(j, h, sc[t, at, :], dp[t, at, :], inv, dd[at, 0:1] * inv)
                key_side(j, t)
                oa[j] += mm(pb[j], vs[pl.ds(start, TILE), :], NN)
                qa[j] += mm(db[j], ks[pl.ds(start, TILE), :], NN)
                return c

            count = wins[j][2]
            lax.fori_loop(0, count, first_pass, 0)
            lax.fori_loop(0, count, second_pass, 0)
            lax.fori_loop(0, count, third_pass, 0)

    for m in range(n):
        for j in range(spans_own):
            at = place(m, j)
            to = slice(j * span, (j + 1) * span)
            parts[m][to, 0:DH] = (dk[pl.ds(at, span), :] * SCALE).astype(parts[m].dtype)
            parts[m][to, DH : 2 * DH] = dv[pl.ds(at, span), :].astype(parts[m].dtype)


def back_kernel(n, heads, span, spans_all, docs, meta, *refs):
    pb, db, kw, vw, oa, qa, att_ref, dq_ref = refs
    own, dl, wins, short = plan(meta, n, span, spans_all, docs)
    spans_own = len(wins)

    def store(j, o, dq):
        for h in range(heads):
            at = slice(h * span, (h + 1) * span)
            to = (slice(j * span, (j + 1) * span), slice(h * DH, (h + 1) * DH))
            att_ref[to] = o[at, :].astype(att_ref.dtype)
            dq_ref[to] = (dq[at, :] * SCALE).astype(dq_ref.dtype)

    @pl.when(short)
    def _():
        for j in range(spans_own):
            store(j, mm(pb[j], vw[j], NN), mm(db[j], kw[j], NN))

    @pl.when(jnp.logical_not(short))
    def _():
        for j in range(spans_own):
            store(j, oa[j], qa[j])


def merge_kernel(a, b, c, key_ref, value_ref):
    total = a[...].astype(jnp.float32) + b[...].astype(jnp.float32) + c[...].astype(jnp.float32)
    key_ref[...] = total[:, :DH].astype(key_ref.dtype)
    value_ref[...] = total[:, DH:].astype(value_ref.dtype)


def local(queries, key_vectors, value_vectors, out_grad, span_order, doc_lengths):
    tok, width = queries.shape
    n = lax.axis_size("ctx")
    heads = width // DH
    spans_all = span_order.shape[0]
    spans_own = spans_all // n
    docs = doc_lengths.shape[0]
    seq = tok * n
    span = seq // spans_all
    rows = heads * span
    tiles = max(spans_own, -(-seq // TILE))
    bits = [1 << b for b in range(n.bit_length() - 1)]
    bf, f32 = jnp.bfloat16, jnp.float32

    def swap(x, m):
        return lax.ppermute(x, "ctx", [(i, i ^ m) for i in range(n)])

    vm = pl.BlockSpec(memory_space=pltpu.VMEM)
    sm = pl.BlockSpec(memory_space=pltpu.SMEM)
    S = jax.ShapeDtypeStruct
    V = pltpu.VMEM
    sizes = (n, heads, span, spans_all, docs)

    def prepare(*refs):
        prepare_kernel(*sizes, *refs)

    def front(*refs):
        front_kernel(*sizes, *refs)

    def back(*refs):
        back_kernel(*sizes, *refs)

    part = [S((tok, 2 * DH), bf if m % 2 else f32) for m in range(n)]
    middle = [
        S((spans_own, rows, TILE), bf),
        S((spans_own, rows, TILE), bf),
        S((spans_own, TILE, DH), bf),
        S((spans_own, TILE, DH), bf),
        S((spans_own, rows, DH), f32),
        S((spans_own, rows, DH), f32),
    ]
    def side(a, b, axis):
        before = [(0, 0)] * a.ndim
        after = [(0, 0)] * a.ndim
        before[axis] = (a.shape[axis], 0)
        after[axis] = (0, b.shape[axis])
        return jnp.pad(a, after) + jnp.pad(b, before)

    kv = {0: side(key_vectors, value_vectors, 1)}
    meta = side(span_order, doc_lengths, 0)
    for bit in reversed(bits):
        for m in list(kv):
            with jax.named_scope("hop%d" % bit):
                kv[m | bit] = swap(kv[m], bit)
    qs, gs, bias = pl.pallas_call(
        prepare,
        out_shape=[
            S((spans_own, rows, DH), bf),
            S((spans_own, rows, DH), bf),
            S((spans_own, span, TILE), f32),
        ],
        in_specs=[sm, vm],
        out_specs=[vm, vm, vm],
        compiler_params=pltpu.CompilerParams(vmem_limit_bytes=8 << 20),
        name="prepare",
    )(meta, side(queries, out_grad, 0))
    res = pl.pallas_call(
        front,
        out_shape=part + middle,
        in_specs=[sm] + [vm] * (3 + n),
        out_specs=[vm] * (n + 6),
        scratch_shapes=[
            V((TILE + seq, DH), bf),
            V((TILE + seq, DH), bf),
            V((TILE + seq, DH), f32),
            V((TILE + seq, DH), f32),
            V((tiles, rows, TILE), f32),
            V((tiles, rows, TILE), f32),
            V((rows, DH), f32),
            V((rows, DH), f32),
            V((rows, DH), f32),
            V((span, TILE), f32),
        ],
        compiler_params=pltpu.CompilerParams(vmem_limit_bytes=(16 + 3 * tiles) << 20),
        name="front",
    )(meta, qs, gs, bias, *[kv[m] for m in range(n)])
    attended, query_grad = pl.pallas_call(
        back,
        out_shape=[S((tok, width), bf), S((tok, width), bf)],
        in_specs=[sm] + [vm] * 6,
        out_specs=[vm, vm],
        compiler_params=pltpu.CompilerParams(vmem_limit_bytes=16 << 20),
        name="back",
    )(meta, *res[n:])

    held = {m: [res[m]] for m in range(n)}
    for bit in bits:
        for m in sorted(held, reverse=True):
            if m & bit:
                mine = held.pop(m)
                block = mine[0].astype(f32)
                for other in mine[1:]:
                    block = block + other.astype(f32)
                held[m ^ bit].append(swap(block.astype(bf), bit))
    terms = held[0]
    while len(terms) > 3:
        terms = [terms[0].astype(f32) + terms[1].astype(f32)] + terms[2:]
    half = S((tok, DH), bf)
    key_grad, value_grad = pl.pallas_call(
        merge_kernel,
        out_shape=[half, half],
        in_specs=[vm] * 3,
        out_specs=[vm, vm],
        compiler_params=pltpu.CompilerParams(vmem_limit_bytes=4 << 20),
        name="merge",
    )(*terms)
    return attended, query_grad, key_grad, value_grad


def solution(mesh):
    rows = P(("seq", "ctx"), None)
    return jax.shard_map(
        local,
        mesh=mesh,
        in_specs=(rows, rows, rows, rows, P("seq"), P("seq")),
        out_specs=(rows, rows, rows, rows),
        check_vma=False,
    )
```

time: 24.9 us -> 19 us (0.76)
  waiting for transfers between devices: 9.94 us -> 3.76 us
  local copies, waits for them, and re-layouts: 2.84 us -> 0.01 us
  other arithmetic: 0 us -> 2.11 us
  Pallas kernels: 5.62 us -> 6.75 us
    ppermute x6, waiting for transfers between devices: 9.94 us -> 3.76 us  [swap(): return lax.ppermute(x, 'ctx', [(i, i ^ m) for i in range(n)])]
    unnamed x11 -> x4, local copies, waits for them, and re-layouts: 2.82 us -> 0.01 us
    add x0 -> x3, other arithmetic: none -> 2.09 us  [side(): return jnp.pad(a, after) + jnp.pad(b, before)]
    pallas_call x2 -> x4, Pallas kernels: 5.62 us -> 6.75 us  [the longest x1 3.13 us: local(): pl.pallas_call(front, out_shape=part + middle, in_specs=[sm] + [vm] * (3...]
  transfers between devices with their start and end apart: 6 -> 6, of which waited for: 4 -> 4; matrix products, arithmetic and copies ran while one was open for 0% -> 7% of each run, Pallas kernels for 0% -> 16%
where the time goes in v2:
time: 19 us; the launch traced here: 18.8 us
  Pallas kernels  6.75 us (36%)
  starting transfers between devices  5.51 us (29%)
  waiting for transfers between devices  3.76 us (20%)
  other arithmetic  2.11 us (11%)
  between operations  0.69 us (4%)
    ppermute x6, starting transfers between devices, swap(): return lax.ppermute(x, 'ctx', [(i, i ^ m) for i in range(n)])  5.51 us
    ppermute x6, waiting for transfers between devices, swap(): return lax.ppermute(x, 'ctx', [(i, i ^ m) for i in range(n)])  3.76 us
    pallas_call x1, Pallas kernels, local(): pl.pallas_call(front, out_shape=part + middle, in_specs=[sm] + [vm] * (3...  3.13 us
    pallas_call x1, Pallas kernels, local(): pl.pallas_call(back, out_shape=[S((tok, width), bf), S((tok, width), bf)]...  2.23 us
    add x3, other arithmetic, side(): return jnp.pad(a, after) + jnp.pad(b, before)  2.09 us
    pallas_call x1, Pallas kernels, local(): pl.pallas_call(prepare, out_shape=[S((spans_own, rows, DH), bf), S((spans...  0.73 us
    pallas_call x1, Pallas kernels, local(): pl.pallas_call(merge_kernel, out_shape=[half, half], in_specs=[vm] * 3, o...  0.66 us
  transfers between devices with their start and end apart: 6, of which 4 were waited for; matrix products, arithmetic and copies ran while one was open for 7% of the time, Pallas kernels for 16%

profile of v2, /device:TPU:0, one launch (start us, length us, event | category | flops | bytes accessed | tf_op | source)
XLA Modules:
  0.0 18.8 jit_solution(6860169502255156734)
XLA Ops:
  0.6 0.0 copy-start
  0.6 0.0 copy-start.1
  0.7 0.8 %pad_add_fusion.1.refs_4_ = bf16[192,256]{1,0:T(8,128)(2,1)S(1)} fusion(bf16[192,128]{1,0:T(8,128)(2,1)} %param.8, bf16[192,128]{1,0:T(8,128)(2,1)} %param.7), kind=kLoop, calls=%fused_computation.2 | loop fusion | flops 196608 | bytes 196608 | tf_op jit(solution)/shard_map/add | solution.py:252
  1.5 3.0 %collective-permute-start.1 = (bf16[192,256]{1,0:T(8,128)(2,1)S(1)}, bf16[192,256]{1,0:T(8,128)(2,1)S(1)}, u32[]{:S(2)}, u32[]{:S(2)}) collective-permute-start(bf16[192,256]{1,0:T(8,128)(2,1)S(1)} %pad_add_fusion.1.refs_4_), channel_id=1, source_target_pairs={{0,16},{8,24},{16,0},{24,8},{1,17},{9,25},{17,1},{25,9},{2,18},{10... | collective-permute-start | bytes 294920 | tf_op jit(solution)/shard_map/hop2/ppermute | solution.py:221
  4.5 0.0 collective-permute-start
  4.5 1.2 %pad_add_fusion.refs_1_ = bf16[384,1024]{1,0:T(8,128)(2,1)S(1)} fusion(bf16[192,1024]{1,0:T(8,128)(2,1)} %param.9, bf16[192,1024]{1,0:T(8,128)(2,1)} %param.6), kind=kLoop, calls=%fused_computation | loop fusion | flops 1572864 | bytes 1572864 | tf_op jit(solution)/shard_map/add | solution.py:252
  5.7 1.6 %collective-permute-done.1.refs_6_ = bf16[192,256]{1,0:T(8,128)(2,1)S(1)} collective-permute-done((bf16[192,256]{1,0:T(8,128)(2,1)S(1)}, bf16[192,256]{1,0:T(8,128)(2,1)S(1)}, u32[]{:S(2)}, u32[]{:S(2)}) %collective-permute-start.1) | collective-permute-done | bytes 98336 | tf_op jit(solution)/shard_map/hop2/ppermute | solution.py:221
  7.3 0.0 collective-permute-start.2
  7.3 0.0 copy-done
  7.3 0.0 copy-done.1
  7.3 0.1 pad_add_fusion.2.refs_0_
  7.4 0.7 %prepare.1 = (bf16[2,768,128]{2,1,0:T(8,128)(2,1)S(1)}, bf16[2,768,128]{2,1,0:T(8,128)(2,1)S(1)}, f32[2,96,384]{2,1,0:T(8,128)S(1)}) custom-call(s32[14]{0:T(128)S(1)} %pad_add_fusion.2.refs_0_, bf16[384,1024]{1,0:T(8,128)(2,1)S(1)} %pad_add_fusion.refs_1_), custom_call_target="tpu_custom_call" | custom-call | tf_op jit(solution)/shard_map/prepare/pallas_call | solution.py:260
  8.2 0.0 collective-permute-done.refs_5_
  8.2 0.5 %collective-permute-done.2.refs_7_ = bf16[192,256]{1,0:T(8,128)(2,1)S(1)} collective-permute-done((bf16[192,256]{1,0:T(8,128)(2,1)S(1)}, bf16[192,256]{1,0:T(8,128)(2,1)S(1)}, u32[]{:S(2)}, u32[]{:S(2)}) %collective-permute-start.2) | collective-permute-done | bytes 98336 | tf_op jit(solution)/shard_map/hop1/ppermute | solution.py:221
  8.6 3.1 %front.1 = (f32[192,256]{1,0:T(8,128)S(1)}, bf16[192,256]{1,0:T(8,128)(2,1)S(1)}, f32[192,256]{1,0:T(8,128)S(1)}, bf16[192,256]{1,0:T(8,128)(2,1)S(1)}, bf16[2,7...) custom-call(s32[14]{0:T(128)S(1)} %pad_add_fusion.2.refs_0_, ...), custom_call_target="tpu_custom_call" | custom-call | tf_op jit(solution)/shard_map/front/pallas_call | solution.py:272
  11.8 0.2 %collective-permute-start.4 = (bf16[192,256]{1,0:T(8,128)(2,1)S(1)}, bf16[192,256]{1,0:T(8,128)(2,1)S(1)}, u32[]{:S(2)}, u32[]{:S(2)}) collective-permute-start(bf16[192,256]{1,0:T(8,128)(2,1)S(1)} %get-tuple-element.35), channel_id=1, source_target_pairs={{0,8},{8,0},{16,24},{24,16},{1,9},{9,1},{17,25},{25,17},{2,10},{10... | collective-permute-start | bytes 294920 | tf_op jit(solution)/shard_map/ppermute | solution.py:221
  12.0 0.4 %collective-permute-start.3 = (bf16[192,256]{1,0:T(8,128)(2,1)S(1)}, bf16[192,256]{1,0:T(8,128)(2,1)S(1)}, u32[]{:S(2)}, u32[]{:S(2)}) collective-permute-start(bf16[192,256]{1,0:T(8,128)(2,1)S(1)} %get-tuple-element.33), channel_id=1, source_target_pairs={{0,8},{8,0},{16,24},{24,16},{1,9},{9,1},{17,25},{25,17},{2,10},{10... | collective-permute-start | bytes 294920 | tf_op jit(solution)/shard_map/ppermute | solution.py:221
  12.3 0.8 %collective-permute-done.4 = bf16[192,256]{1,0:T(8,128)(2,1)S(1)} collective-permute-done((bf16[192,256]{1,0:T(8,128)(2,1)S(1)}, bf16[192,256]{1,0:T(8,128)(2,1)S(1)}, u32[]{:S(2)}, u32[]{:S(2)}) %collective-permute-start.4) | collective-permute-done | bytes 98336 | tf_op jit(solution)/shard_map/ppermute | solution.py:221
  13.2 1.9 %collective-permute-start.5 = (bf16[192,256]{1,0:T(8,128)(2,1)S(1)}, bf16[192,256]{1,0:T(8,128)(2,1)S(1)}, u32[]{:S(2)}, u32[]{:S(2)}) collective-permute-start(bf16[192,256]{1,0:T(8,128)(2,1)S(1)} %add_convert_fusion), channel_id=1, source_target_pairs={{0,16},{8,24},{16,0},{24,8},{1,17},{9,25},{17,1},{25,9},{2,18},{10... | collective-permute-start | bytes 294920 | tf_op jit(solution)/shard_map/ppermute | solution.py:221
  15.1 2.2 %back.1 = (bf16[192,1024]{1,0:T(8,128)(2,1)}, bf16[192,1024]{1,0:T(8,128)(2,1)}) custom-call(s32[14]{0:T(128)S(1)} %pad_add_fusion.2.refs_0_, bf16[2,768,384]{2,1,0:T(8,128)(2,1)S(1)} %get-tuple-element.24.refs_1_, bf16[2,768,384]{2,1,0:T(8,128)(2,1)S(1)} %get-tuple-element.25.refs_2_, bf16[2,384,128]{2,1,0:T(8,128)(2,1)S(1)} %get-tuple-element.26.refs_3_, ...), custom_call_target="tpu_custom_call" | custom-call | tf_op jit(solution)/shard_map/back/pallas_call | solution.py:292
  17.3 0.0 collective-permute-done.3.b
  17.3 0.9 %collective-permute-done.5.c = bf16[192,256]{1,0:T(8,128)(2,1)S(1)} collective-permute-done((bf16[192,256]{1,0:T(8,128)(2,1)S(1)}, bf16[192,256]{1,0:T(8,128)(2,1)S(1)}, u32[]{:S(2)}, u32[]{:S(2)}) %collective-permute-start.5) | collective-permute-done | bytes 98336 | tf_op jit(solution)/shard_map/ppermute | solution.py:221
  18.2 0.7 %merge.1 = (bf16[192,128]{1,0:T(8,128)(2,1)}, bf16[192,128]{1,0:T(8,128)(2,1)}) custom-call(f32[192,256]{1,0:T(8,128)S(1)} %get-tuple-element.32.a, bf16[192,256]{1,0:T(8,128)(2,1)S(1)} %collective-permute-done.3.b, bf16[192,256]{1,0:T(8,128)(2,1)S(1)} %collective-permute-done.5.c), custom_call_target="tpu_custom_call" | custom-call | tf_op jit(solution)/shard_map/merge/pallas_call | solution.py:314
  (1 shorter events, 0.0 us)
Async XLA Ops:
  0.6 6.7 %copy-start = (s32[6]{0:T(128)S(1)}, s32[6]{0:T(128)}, u32[]{:S(2)}) copy-start(s32[6]{0:T(128)} %param.11) | copy-start | bytes 76
  0.6 6.7 %copy-start.1 = (s32[8]{0:T(128)S(1)}, s32[8]{0:T(128)}, u32[]{:S(2)}) copy-start(s32[8]{0:T(128)} %param.10) | copy-start | bytes 100
  1.5 5.8 %collective-permute-start.1 = (bf16[192,256]{1,0:T(8,128)(2,1)S(1)}, bf16[192,256]{1,0:T(8,128)(2,1)S(1)}, u32[]{:S(2)}, u32[]{:S(2)}) collective-permute-start(bf16[192,256]{1,0:T(8,128)(2,1)S(1)} %pad_add_fusion.1.refs_4_), channel_id=1, source_target_pairs={{0,16},{8,24},{16,0},{24,8},{1,17},{9,25},{17,1},{25,9},{2,18},{10... | collective-permute-start | bytes 294920 | tf_op jit(solution)/shard_map/hop2/ppermute | solution.py:221
  4.5 3.6 %collective-permute-start = (bf16[192,256]{1,0:T(8,128)(2,1)S(1)}, bf16[192,256]{1,0:T(8,128)(2,1)S(1)}, u32[]{:S(2)}, u32[]{:S(2)}) collective-permute-start(bf16[192,256]{1,0:T(8,128)(2,1)S(1)} %pad_add_fusion.1.refs_4_), channel_id=1, source_target_pairs={{0,8},{8,0},{16,24},{24,16},{1,9},{9,1},{17,25},{25,17},{2,10},{10... | collective-permute-start | bytes 294920 | tf_op jit(solution)/shard_map/hop1/ppermute | solution.py:221
  7.3 1.3 %collective-permute-start.2 = (bf16[192,256]{1,0:T(8,128)(2,1)S(1)}, bf16[192,256]{1,0:T(8,128)(2,1)S(1)}, u32[]{:S(2)}, u32[]{:S(2)}) collective-permute-start(bf16[192,256]{1,0:T(8,128)(2,1)S(1)} %collective-permute-done.1.refs_6_), channel_id=1, source_target_pairs={{0,8},{8,0},{16,24},{24,16},{1,9},{9,1},{17,25},{25,17},{2,10},{10... | collective-permute-start | bytes 294920 | tf_op jit(solution)/shard_map/hop1/ppermute | solution.py:221
  11.8 1.4 %collective-permute-start.4 = (bf16[192,256]{1,0:T(8,128)(2,1)S(1)}, bf16[192,256]{1,0:T(8,128)(2,1)S(1)}, u32[]{:S(2)}, u32[]{:S(2)}) collective-permute-start(bf16[192,256]{1,0:T(8,128)(2,1)S(1)} %get-tuple-element.35), channel_id=1, source_target_pairs={{0,8},{8,0},{16,24},{24,16},{1,9},{9,1},{17,25},{25,17},{2,10},{10... | collective-permute-start | bytes 294920 | tf_op jit(solution)/shard_map/ppermute | solution.py:221
  12.0 5.3 %collective-permute-start.3 = (bf16[192,256]{1,0:T(8,128)(2,1)S(1)}, bf16[192,256]{1,0:T(8,128)(2,1)S(1)}, u32[]{:S(2)}, u32[]{:S(2)}) collective-permute-start(bf16[192,256]{1,0:T(8,128)(2,1)S(1)} %get-tuple-element.33), channel_id=1, source_target_pairs={{0,8},{8,0},{16,24},{24,16},{1,9},{9,1},{17,25},{25,17},{2,10},{10... | collective-permute-start | bytes 294920 | tf_op jit(solution)/shard_map/ppermute | solution.py:221
  13.2 5.0 %collective-permute-start.5 = (bf16[192,256]{1,0:T(8,128)(2,1)S(1)}, bf16[192,256]{1,0:T(8,128)(2,1)S(1)}, u32[]{:S(2)}, u32[]{:S(2)}) collective-permute-start(bf16[192,256]{1,0:T(8,128)(2,1)S(1)} %add_convert_fusion), channel_id=1, source_target_pairs={{0,16},{8,24},{16,0},{24,8},{1,17},{9,25},{17,1},{25,9},{2,18},{10... | collective-permute-start | bytes 294920 | tf_op jit(solution)/shard_map/ppermute | solution.py:221

commit v3 on v2

--- a/solution.py
+++ b/solution.py
@@ -9,6 +9,7 @@
 
 DH = 128
 TILE = 384
+BLOCK = 16
 FILL = -1e30
 SCALE = 1.0 / math.sqrt(DH)
 GROW = SCALE * math.log2(math.e)
@@ -33,20 +34,33 @@
     return first, stop, (stop - begin + TILE - 1) // TILE
 
 
-def plan(meta, n, span, spans_all, docs):
+def unpack(info, n, span, spans_all, docs):
+    spans_own = spans_all // n
+    at = [info[0, i] for i in range(spans_all)]
+    stops = [info[0, spans_all + j] for j in range(spans_own)]
+    counts = [info[0, spans_all + spans_own + j] for j in range(spans_own)]
+    short = counts[0] == 1
+    for c in counts[1:]:
+        short = short & (c == 1)
+    wins = [(stop - span, stop, count) for stop, count in zip(stops, counts)]
+    return at, wins, short
+
+
+def prepare_kernel(n, heads, span, spans_all, docs, meta, both, qs, gs, bias, info, qt, gt):
     own = lax.axis_index("ctx")
     spans_own = spans_all // n
     dl = [meta[spans_all + d] for d in range(docs)]
     wins = [window(meta, dl, own * spans_own + j, span, docs) for j in range(spans_own)]
-    short = wins[0][2] == 1
-    for w in wins[1:]:
-        short = short & (w[2] == 1)
-    return own, dl, wins, short
-
-
-def prepare_kernel(n, heads, span, spans_all, docs, meta, both, qs, gs, bias):
-    own, dl, wins, short = plan(meta, n, span, spans_all, docs)
-    tok = len(wins) * span
+    tok = spans_own * span
+    values = [
+        meta[(own ^ m) * spans_own + j] * span + TILE for m in range(n) for j in range(spans_own)
+    ]
+    values += [w[1] for w in wins] + [w[2] for w in wins] + dl
+    lane = lax.broadcasted_iota(jnp.int32, info.shape, 1)
+    packed = jnp.zeros(info.shape, jnp.int32)
+    for i, value in enumerate(values):
+        packed = jnp.where(lane == i, value, packed)
+    info[...] = packed
     for j, (first, stop, count) in enumerate(wins):
         for h in range(heads):
             to = slice(h * span, (h + 1) * span)
@@ -54,6 +68,8 @@
             qs[j, to, :] = both[j * span : (j + 1) * span, cols]
             gs[j, to, :] = both[tok + j * span : tok + (j + 1) * span, cols]
         bias[j] = bias_tile(dl, docs, span, first, stop)
+        qt[j] = qs[j].T
+        gt[j] = gs[j].T
 
 
 def bias_tile(dl, docs, span, first, tile_stop):
@@ -67,8 +83,8 @@
     return jnp.where((key_pos <= pos) & (key_pos >= begin_row), 0.0, FILL)
 
 
-def front_kernel(n, heads, span, spans_all, docs, meta, qs, gs, bias, *refs):
-    own, dl, wins, short = plan(meta, n, span, spans_all, docs)
+def front_kernel(n, heads, span, spans_all, docs, info, qs, gs, bias, qt, gt, *refs):
+    spots, wins, short = unpack(info, n, span, spans_all, docs)
     spans_own = spans_all // n
     kv = refs[0:n]
     parts = refs[n : 2 * n]
@@ -82,7 +98,7 @@
     dv[...] = jnp.zeros(dv.shape, dv.dtype)
 
     def place(m, j):
-        return pl.multiple_of(meta[(own ^ m) * spans_own + j] * span + pad, 16)
+        return pl.multiple_of(spots[m * spans_own + j], 16)
 
     for m in range(n):
         for j in range(spans_own):
@@ -93,15 +109,15 @@
     def tile_at(j, t):
         return pl.multiple_of(wins[j][1] + pad - (t + 1) * TILE, 16)
 
-    def finish(j, h, e, grads, inv, mean):
+    def finish(j, at, e, grads, inv, mean):
         p = e * inv
-        pb[j, head_rows[h], :] = p.astype(jnp.bfloat16)
-        db[j, head_rows[h], :] = (p * (grads - mean)).astype(jnp.bfloat16)
+        pb[j, at, :] = p.astype(jnp.bfloat16)
+        db[j, at, :] = (p * (grads - mean)).astype(jnp.bfloat16)
 
     def key_side(j, t):
         start = tile_at(j, t)
-        dv[pl.ds(start, TILE), :] += mm(pb[j], gs[j], TN)
-        dk[pl.ds(start, TILE), :] += mm(db[j], qs[j], TN)
+        dv[pl.ds(start, TILE), :] += mm(gt[j], pb[j], NN).T
+        dk[pl.ds(start, TILE), :] += mm(qt[j], db[j], NN).T
 
     @pl.when(short)
     def _():
@@ -112,18 +128,20 @@
         for j in range(spans_own):
             sc[j] = mm(qs[j], kw[j], NT)
             dp[j] = mm(gs[j], vw[j], NT)
-            for h in range(heads):
-                s = sc[j, head_rows[h], :] + bias[j]
+            for r in range(0, heads * span, BLOCK):
+                at = slice(r, r + BLOCK)
+                s = sc[j, at, :] + bias[j, r % span : r % span + BLOCK, :]
                 e = jnp.exp2((s - jnp.max(s, axis=1, keepdims=True)) * GROW)
-                grads = dp[j, head_rows[h], :]
+                grads = dp[j, at, :]
                 inv = 1.0 / jnp.sum(e, axis=1, keepdims=True)
                 mean = jnp.sum(e * grads, axis=1, keepdims=True) * inv
-                finish(j, h, e, grads, inv, mean)
+                finish(j, at, e, grads, inv, mean)
         for j in range(spans_own):
             key_side(j, 0)
 
     @pl.when(jnp.logical_not(short))
     def _():
+        dl = [info[0, spans_all + 2 * spans_own + d] for d in range(docs)]
         for j in range(spans_own):
             mx[...] = jnp.full(mx.shape, FILL, mx.dtype)
             ls[...] = jnp.zeros(ls.shape, ls.dtype)
@@ -152,10 +170,9 @@
 
             def third_pass(t, c):
                 start = tile_at(j, t)
-                for h in range(heads):
-                    at = head_rows[h]
+                for at in head_rows:
                     inv = 1.0 / ls[at, 0:1]
-                    finish(j, h, sc[t, at, :], dp[t, at, :], inv, dd[at, 0:1] * inv)
+                    finish(j, at, sc[t, at, :], dp[t, at, :], inv, dd[at, 0:1] * inv)
                 key_side(j, t)
                 oa[j] += mm(pb[j], vs[pl.ds(start, TILE), :], NN)
                 qa[j] += mm(db[j], ks[pl.ds(start, TILE), :], NN)
@@ -174,9 +191,9 @@
             parts[m][to, DH : 2 * DH] = dv[pl.ds(at, span), :].astype(parts[m].dtype)
 
 
-def back_kernel(n, heads, span, spans_all, docs, meta, *refs):
+def back_kernel(n, heads, span, spans_all, docs, info, *refs):
     pb, db, kw, vw, oa, qa, att_ref, dq_ref = refs
-    own, dl, wins, short = plan(meta, n, span, spans_all, docs)
+    unused, wins, short = unpack(info, n, span, spans_all, docs)
     spans_own = len(wins)
 
     def store(j, o, dq):
@@ -257,22 +274,25 @@
         for m in list(kv):
             with jax.named_scope("hop%d" % bit):
                 kv[m | bit] = swap(kv[m], bit)
-    qs, gs, bias = pl.pallas_call(
+    qs, gs, bias, info, qt, gt = pl.pallas_call(
         prepare,
         out_shape=[
             S((spans_own, rows, DH), bf),
             S((spans_own, rows, DH), bf),
             S((spans_own, span, TILE), f32),
+            S((8, 128 * -(-(spans_all + 2 * spans_own + docs) // 128)), jnp.int32),
+            S((spans_own, DH, rows), bf),
+            S((spans_own, DH, rows), bf),
         ],
         in_specs=[sm, vm],
-        out_specs=[vm, vm, vm],
+        out_specs=[vm] * 6,
         compiler_params=pltpu.CompilerParams(vmem_limit_bytes=8 << 20),
         name="prepare",
     )(meta, side(queries, out_grad, 0))
     res = pl.pallas_call(
         front,
         out_shape=part + middle,
-        in_specs=[sm] + [vm] * (3 + n),
+        in_specs=[vm] * (6 + n),
         out_specs=[vm] * (n + 6),
         scratch_shapes=[
             V((TILE + seq, DH), bf),
@@ -288,15 +308,15 @@
         ],
         compiler_params=pltpu.CompilerParams(vmem_limit_bytes=(16 + 3 * tiles) << 20),
         name="front",
-    )(meta, qs, gs, bias, *[kv[m] for m in range(n)])
+    )(info, qs, gs, bias, qt, gt, *[kv[m] for m in range(n)])
     attended, query_grad = pl.pallas_call(
         back,
         out_shape=[S((tok, width), bf), S((tok, width), bf)],
-        in_specs=[sm] + [vm] * 6,
+        in_specs=[vm] * 7,
         out_specs=[vm, vm],
         compiler_params=pltpu.CompilerParams(vmem_limit_bytes=16 << 20),
         name="back",
-    )(meta, *res[n:])
+    )(info, *res[n:])
 
     held = {m: [res[m]] for m in range(n)}
     for bit in bits:

time: 19 us -> 18.2 us (0.958)
  Pallas kernels: 6.75 us -> 5.6 us
  waiting for transfers between devices: 3.76 us -> 4.14 us
    pallas_call x1, Pallas kernels: 3.13 us -> 2.34 us  [local(): pl.pallas_call(front, out_shape=part + middle, in_specs=[vm] * (6 + n), o...]
    pallas_call x1, Pallas kernels: 2.23 us -> 1.75 us  [local(): pl.pallas_call(back, out_shape=[S((tok, width), bf), S((tok, width), bf)]...]
    ppermute x6, waiting for transfers between devices: 3.76 us -> 4.14 us  [swap(): return lax.ppermute(x, 'ctx', [(i, i ^ m) for i in range(n)])]
  transfers between devices with their start and end apart: 6 -> 6, of which waited for: 4 -> 4; matrix products, arithmetic and copies ran while one was open for 7% -> 7% of each run, Pallas kernels for 16% -> 14%
where the time goes in v3:
time: 18.2 us; the launch traced here: 18 us
  Pallas kernels  5.6 us (31%)
  starting transfers between devices  5.5 us (30%)
  waiting for transfers between devices  4.14 us (23%)
  other arithmetic  2.11 us (12%)
  between operations  0.69 us (4%)
    ppermute x6, starting transfers between devices, swap(): return lax.ppermute(x, 'ctx', [(i, i ^ m) for i in range(n)])  5.5 us
    ppermute x6, waiting for transfers between devices, swap(): return lax.ppermute(x, 'ctx', [(i, i ^ m) for i in range(n)])  4.14 us
    pallas_call x1, Pallas kernels, local(): pl.pallas_call(front, out_shape=part + middle, in_specs=[vm] * (6 + n), o...  2.34 us
    add x3, other arithmetic, side(): return jnp.pad(a, after) + jnp.pad(b, before)  2.09 us
    pallas_call x1, Pallas kernels, local(): pl.pallas_call(back, out_shape=[S((tok, width), bf), S((tok, width), bf)]...  1.75 us
    pallas_call x1, Pallas kernels, local(): pl.pallas_call(prepare, out_shape=[S((spans_own, rows, DH), bf), S((spans...  0.84 us
    pallas_call x1, Pallas kernels, local(): pl.pallas_call(merge_kernel, out_shape=[half, half], in_specs=[vm] * 3, o...  0.66 us
  transfers between devices with their start and end apart: 6, of which 4 were waited for; matrix products, arithmetic and copies ran while one was open for 7% of the time, Pallas kernels for 14%

profile of v3, /device:TPU:0, one launch (start us, length us, event | category | flops | bytes accessed | tf_op | source)
XLA Modules:
  0.0 18.0 jit_solution(10009048020011523259)
XLA Ops:
  0.6 0.0 copy-start
  0.6 0.0 copy-start.1
  0.7 0.8 %pad_add_fusion.1.refs_6_ = bf16[192,256]{1,0:T(8,128)(2,1)S(1)} fusion(bf16[192,128]{1,0:T(8,128)(2,1)} %param.8, bf16[192,128]{1,0:T(8,128)(2,1)} %param.7), kind=kLoop, calls=%fused_computation.2 | loop fusion | flops 196608 | bytes 196608 | tf_op jit(solution)/shard_map/add | solution.py:269
  1.5 3.0 %collective-permute-start.1 = (bf16[192,256]{1,0:T(8,128)(2,1)S(1)}, bf16[192,256]{1,0:T(8,128)(2,1)S(1)}, u32[]{:S(2)}, u32[]{:S(2)}) collective-permute-start(bf16[192,256]{1,0:T(8,128)(2,1)S(1)} %pad_add_fusion.1.refs_6_), channel_id=1, source_target_pairs={{0,16},{8,24},{16,0},{24,8},{1,17},{9,25},{17,1},{25,9},{2,18},{10... | collective-permute-start | bytes 294920 | tf_op jit(solution)/shard_map/hop2/ppermute | solution.py:238
  4.5 0.0 collective-permute-start
  4.5 1.2 %pad_add_fusion.refs_1_ = bf16[384,1024]{1,0:T(8,128)(2,1)S(1)} fusion(bf16[192,1024]{1,0:T(8,128)(2,1)} %param.9, bf16[192,1024]{1,0:T(8,128)(2,1)} %param.6), kind=kLoop, calls=%fused_computation | loop fusion | flops 1572864 | bytes 1572864 | tf_op jit(solution)/shard_map/add | solution.py:269
  5.7 1.6 %collective-permute-done.1.refs_8_ = bf16[192,256]{1,0:T(8,128)(2,1)S(1)} collective-permute-done((bf16[192,256]{1,0:T(8,128)(2,1)S(1)}, bf16[192,256]{1,0:T(8,128)(2,1)S(1)}, u32[]{:S(2)}, u32[]{:S(2)}) %collective-permute-start.1) | collective-permute-done | bytes 98336 | tf_op jit(solution)/shard_map/hop2/ppermute | solution.py:238
  7.3 0.0 collective-permute-start.2
  7.3 0.0 copy-done
  7.3 0.0 copy-done.1
  7.3 0.1 pad_add_fusion.2.refs_0_
  7.4 0.8 %prepare.1 = (bf16[2,768,128]{2,1,0:T(8,128)(2,1)S(1)}, bf16[2,768,128]{2,1,0:T(8,128)(2,1)S(1)}, f32[2,96,384]{2,1,0:T(8,128)S(1)}, s32[8,128]{1,0:T(8,128)S(1)...) custom-call(s32[14]{0:T(128)S(1)} %pad_add_fusion.2.refs_0_, bf16[384,1024]{1,0:T(8,128)(2,1)S(1)} %pad_add_fusion.refs_1_), custom_call_target="tpu_custom_call" | custom-call | tf_op jit(solution)/shard_map/prepare/pallas_call | solution.py:277
  8.3 0.0 collective-permute-done.refs_7_
  8.3 0.4 %collective-permute-done.2.refs_9_ = bf16[192,256]{1,0:T(8,128)(2,1)S(1)} collective-permute-done((bf16[192,256]{1,0:T(8,128)(2,1)S(1)}, bf16[192,256]{1,0:T(8,128)(2,1)S(1)}, u32[]{:S(2)}, u32[]{:S(2)}) %collective-permute-start.2) | collective-permute-done | bytes 98336 | tf_op jit(solution)/shard_map/hop1/ppermute | solution.py:238
  8.6 2.3 %front.1 = (f32[192,256]{1,0:T(8,128)S(1)}, bf16[192,256]{1,0:T(8,128)(2,1)S(1)}, f32[192,256]{1,0:T(8,128)S(1)}, bf16[192,256]{1,0:T(8,128)(2,1)S(1)}, bf16[2,7...) custom-call(s32[8,128]{1,0:T(8,128)S(1)} %get-tuple-element.24.refs_, ...), custom_call_target="tpu_custom_call" | custom-call | tf_op jit(solution)/shard_map/front/pallas_call | solution.py:292
  11.0 0.2 %collective-permute-start.4 = (bf16[192,256]{1,0:T(8,128)(2,1)S(1)}, bf16[192,256]{1,0:T(8,128)(2,1)S(1)}, u32[]{:S(2)}, u32[]{:S(2)}) collective-permute-start(bf16[192,256]{1,0:T(8,128)(2,1)S(1)} %get-tuple-element.41), channel_id=1, source_target_pairs={{0,8},{8,0},{16,24},{24,16},{1,9},{9,1},{17,25},{25,17},{2,10},{10... | collective-permute-start | bytes 294920 | tf_op jit(solution)/shard_map/ppermute | solution.py:238
  11.2 0.4 %collective-permute-start.3 = (bf16[192,256]{1,0:T(8,128)(2,1)S(1)}, bf16[192,256]{1,0:T(8,128)(2,1)S(1)}, u32[]{:S(2)}, u32[]{:S(2)}) collective-permute-start(bf16[192,256]{1,0:T(8,128)(2,1)S(1)} %get-tuple-element.39), channel_id=1, source_target_pairs={{0,8},{8,0},{16,24},{24,16},{1,9},{9,1},{17,25},{25,17},{2,10},{10... | collective-permute-start | bytes 294920 | tf_op jit(solution)/shard_map/ppermute | solution.py:238
  11.6 0.8 %collective-permute-done.4 = bf16[192,256]{1,0:T(8,128)(2,1)S(1)} collective-permute-done((bf16[192,256]{1,0:T(8,128)(2,1)S(1)}, bf16[192,256]{1,0:T(8,128)(2,1)S(1)}, u32[]{:S(2)}, u32[]{:S(2)}) %collective-permute-start.4) | collective-permute-done | bytes 98336 | tf_op jit(solution)/shard_map/ppermute | solution.py:238
  12.4 1.9 %collective-permute-start.5 = (bf16[192,256]{1,0:T(8,128)(2,1)S(1)}, bf16[192,256]{1,0:T(8,128)(2,1)S(1)}, u32[]{:S(2)}, u32[]{:S(2)}) collective-permute-start(bf16[192,256]{1,0:T(8,128)(2,1)S(1)} %add_convert_fusion), channel_id=1, source_target_pairs={{0,16},{8,24},{16,0},{24,8},{1,17},{9,25},{17,1},{25,9},{2,18},{10... | collective-permute-start | bytes 294920 | tf_op jit(solution)/shard_map/ppermute | solution.py:238
  14.3 1.8 %back.1 = (bf16[192,1024]{1,0:T(8,128)(2,1)}, bf16[192,1024]{1,0:T(8,128)(2,1)}) custom-call(s32[8,128]{1,0:T(8,128)S(1)} %get-tuple-element.24.refs_0_, bf16[2,768,384]{2,1,0:T(8,128)(2,1)S(1)} %get-tuple-element.30.refs_1_, bf16[2,768,384]{2,1,0:T(8,128)(2,1)S(1)} %get-tuple-element.31.refs_2_, bf16[2,384,128]{2,1,0:T(8,128)(2,1)S(1)} %get-tuple-element.32.refs_3_, ...), custom_call_target="tpu_custom_call" | custom-call | tf_op jit(solution)/shard_map/back/pallas_call | solution.py:312
  16.0 0.0 collective-permute-done.3.b
  16.0 1.4 %collective-permute-done.5.c = bf16[192,256]{1,0:T(8,128)(2,1)S(1)} collective-permute-done((bf16[192,256]{1,0:T(8,128)(2,1)S(1)}, bf16[192,256]{1,0:T(8,128)(2,1)S(1)}, u32[]{:S(2)}, u32[]{:S(2)}) %collective-permute-start.5) | collective-permute-done | bytes 98336 | tf_op jit(solution)/shard_map/ppermute | solution.py:238
  17.4 0.7 %merge.1 = (bf16[192,128]{1,0:T(8,128)(2,1)}, bf16[192,128]{1,0:T(8,128)(2,1)}) custom-call(f32[192,256]{1,0:T(8,128)S(1)} %get-tuple-element.38.a, bf16[192,256]{1,0:T(8,128)(2,1)S(1)} %collective-permute-done.3.b, bf16[192,256]{1,0:T(8,128)(2,1)S(1)} %collective-permute-done.5.c), custom_call_target="tpu_custom_call" | custom-call | tf_op jit(solution)/shard_map/merge/pallas_call | solution.py:334
  (1 shorter events, 0.0 us)
Async XLA Ops:
  0.6 6.7 %copy-start = (s32[6]{0:T(128)S(1)}, s32[6]{0:T(128)}, u32[]{:S(2)}) copy-start(s32[6]{0:T(128)} %param.11) | copy-start | bytes 76
  0.6 6.7 %copy-start.1 = (s32[8]{0:T(128)S(1)}, s32[8]{0:T(128)}, u32[]{:S(2)}) copy-start(s32[8]{0:T(128)} %param.10) | copy-start | bytes 100
  1.5 5.8 %collective-permute-start.1 = (bf16[192,256]{1,0:T(8,128)(2,1)S(1)}, bf16[192,256]{1,0:T(8,128)(2,1)S(1)}, u32[]{:S(2)}, u32[]{:S(2)}) collective-permute-start(bf16[192,256]{1,0:T(8,128)(2,1)S(1)} %pad_add_fusion.1.refs_6_), channel_id=1, source_target_pairs={{0,16},{8,24},{16,0},{24,8},{1,17},{9,25},{17,1},{25,9},{2,18},{10... | collective-permute-start | bytes 294920 | tf_op jit(solution)/shard_map/hop2/ppermute | solution.py:238
  4.5 3.7 %collective-permute-start = (bf16[192,256]{1,0:T(8,128)(2,1)S(1)}, bf16[192,256]{1,0:T(8,128)(2,1)S(1)}, u32[]{:S(2)}, u32[]{:S(2)}) collective-permute-start(bf16[192,256]{1,0:T(8,128)(2,1)S(1)} %pad_add_fusion.1.refs_6_), channel_id=1, source_target_pairs={{0,8},{8,0},{16,24},{24,16},{1,9},{9,1},{17,25},{25,17},{2,10},{10... | collective-permute-start | bytes 294920 | tf_op jit(solution)/shard_map/hop1/ppermute | solution.py:238
  7.3 1.3 %collective-permute-start.2 = (bf16[192,256]{1,0:T(8,128)(2,1)S(1)}, bf16[192,256]{1,0:T(8,128)(2,1)S(1)}, u32[]{:S(2)}, u32[]{:S(2)}) collective-permute-start(bf16[192,256]{1,0:T(8,128)(2,1)S(1)} %collective-permute-done.1.refs_8_), channel_id=1, source_target_pairs={{0,8},{8,0},{16,24},{24,16},{1,9},{9,1},{17,25},{25,17},{2,10},{10... | collective-permute-start | bytes 294920 | tf_op jit(solution)/shard_map/hop1/ppermute | solution.py:238
  11.0 1.4 %collective-permute-start.4 = (bf16[192,256]{1,0:T(8,128)(2,1)S(1)}, bf16[192,256]{1,0:T(8,128)(2,1)S(1)}, u32[]{:S(2)}, u32[]{:S(2)}) collective-permute-start(bf16[192,256]{1,0:T(8,128)(2,1)S(1)} %get-tuple-element.41), channel_id=1, source_target_pairs={{0,8},{8,0},{16,24},{24,16},{1,9},{9,1},{17,25},{25,17},{2,10},{10... | collective-permute-start | bytes 294920 | tf_op jit(solution)/shard_map/ppermute | solution.py:238
  11.2 4.8 %collective-permute-start.3 = (bf16[192,256]{1,0:T(8,128)(2,1)S(1)}, bf16[192,256]{1,0:T(8,128)(2,1)S(1)}, u32[]{:S(2)}, u32[]{:S(2)}) collective-permute-start(bf16[192,256]{1,0:T(8,128)(2,1)S(1)} %get-tuple-element.39), channel_id=1, source_target_pairs={{0,8},{8,0},{16,24},{24,16},{1,9},{9,1},{17,25},{25,17},{2,10},{10... | collective-permute-start | bytes 294920 | tf_op jit(solution)/shard_map/ppermute | solution.py:238
  12.4 5.0 %collective-permute-start.5 = (bf16[192,256]{1,0:T(8,128)(2,1)S(1)}, bf16[192,256]{1,0:T(8,128)(2,1)S(1)}, u32[]{:S(2)}, u32[]{:S(2)}) collective-permute-start(bf16[192,256]{1,0:T(8,128)(2,1)S(1)} %add_convert_fusion), channel_id=1, source_target_pairs={{0,16},{8,24},{16,0},{24,8},{1,17},{9,25},{17,1},{25,9},{2,18},{10... | collective-permute-start | bytes 294920 | tf_op jit(solution)/shard_map/ppermute | solution.py:238

commit v4 on v3

--- a/solution.py
+++ b/solution.py
@@ -46,7 +46,7 @@
     return at, wins, short
 
 
-def prepare_kernel(n, heads, span, spans_all, docs, meta, both, qs, gs, bias, info, qt, gt):
+def prepare_kernel(n, heads, span, spans_all, docs, meta, both, qs, gs, mask, info, qt, gt, dk, dv):
     own = lax.axis_index("ctx")
     spans_own = spans_all // n
     dl = [meta[spans_all + d] for d in range(docs)]
@@ -61,41 +61,45 @@
     for i, value in enumerate(values):
         packed = jnp.where(lane == i, value, packed)
     info[...] = packed
+    wide = qs.shape[2] - DH
+    row = lax.broadcasted_iota(jnp.int32, (span, wide), 0)
+    unit = (row == lax.broadcasted_iota(jnp.int32, (span, wide), 1)).astype(jnp.float32).astype(qs.dtype)
     for j, (first, stop, count) in enumerate(wins):
         for h in range(heads):
             to = slice(h * span, (h + 1) * span)
             cols = slice(h * DH, (h + 1) * DH)
-            qs[j, to, :] = both[j * span : (j + 1) * span, cols]
+            qs[j, to, 0:DH] = both[j * span : (j + 1) * span, cols]
             gs[j, to, :] = both[tok + j * span : tok + (j + 1) * span, cols]
-        bias[j] = bias_tile(dl, docs, span, first, stop)
-        qt[j] = qs[j].T
+            qs[j, to, DH:] = unit
+        qt[j] = qs[j, :, 0:DH].T
         gt[j] = gs[j].T
-
-
-def bias_tile(dl, docs, span, first, tile_stop):
-    pos = first + lax.broadcasted_iota(jnp.int32, (span, TILE), 0)
+        mask[j] = tile_mask(dl, first, stop - TILE, mask.shape[1:], 1).astype(mask.dtype)
+    dk[...] = jnp.zeros(dk.shape, dk.dtype)
+    dv[...] = jnp.zeros(dv.shape, dv.dtype)
+
+
+def tile_mask(dl, first, low, shape, row_axis):
+    pos = first + lax.broadcasted_iota(jnp.int32, shape, row_axis)
+    key_pos = low + lax.broadcasted_iota(jnp.int32, shape, 1 - row_axis)
     edge = jnp.int32(0)
-    begin_row = jnp.zeros((span, TILE), jnp.int32)
-    for d in range(docs):
-        edge = edge + dl[d]
+    begin_row = jnp.zeros(shape, jnp.int32)
+    for length in dl:
+        edge = edge + length
         begin_row = jnp.where(edge <= pos, edge, begin_row)
-    key_pos = lax.broadcasted_iota(jnp.int32, (span, TILE), 1) + (tile_stop - TILE)
     return jnp.where((key_pos <= pos) & (key_pos >= begin_row), 0.0, FILL)
 
 
-def front_kernel(n, heads, span, spans_all, docs, info, qs, gs, bias, qt, gt, *refs):
+def front_kernel(n, heads, span, spans_all, docs, info, qs, gs, mask, qt, gt, zk, zv, *refs):
     spots, wins, short = unpack(info, n, span, spans_all, docs)
     spans_own = spans_all // n
     kv = refs[0:n]
-    parts = refs[n : 2 * n]
-    pb, db, kw, vw, oa, qa = refs[2 * n : 2 * n + 6]
-    ks, vs, dk, dv, sc, dp, mx, ls, dd, more = refs[2 * n + 6 :]
+    parts = refs[n : 2 * n - 1]
+    pb, db, kw, vw, oa, qa, dk, dv = refs[2 * n - 1 : 2 * n + 7]
+    ks, vs, sc, dp, mx, ls, dd, more = refs[2 * n + 7 :]
     pad = TILE
     head_rows = [slice(h * span, (h + 1) * span) for h in range(heads)]
     ks[0:pad, :] = jnp.zeros((pad, DH), ks.dtype)
     vs[0:pad, :] = jnp.zeros((pad, DH), vs.dtype)
-    dk[...] = jnp.zeros(dk.shape, dk.dtype)
-    dv[...] = jnp.zeros(dv.shape, dv.dtype)
 
     def place(m, j):
         return pl.multiple_of(spots[m * spans_own + j], 16)
@@ -123,14 +127,15 @@
     def _():
         for j in range(spans_own):
             start = tile_at(j, 0)
-            kw[j] = ks[pl.ds(start, TILE), :]
+            kw[j, :, 0:DH] = ks[pl.ds(start, TILE), :]
+            kw[j, :, DH:] = mask[j]
             vw[j] = vs[pl.ds(start, TILE), :]
         for j in range(spans_own):
             sc[j] = mm(qs[j], kw[j], NT)
             dp[j] = mm(gs[j], vw[j], NT)
             for r in range(0, heads * span, BLOCK):
                 at = slice(r, r + BLOCK)
-                s = sc[j, at, :] + bias[j, r % span : r % span + BLOCK, :]
+                s = sc[j, at, :]
                 e = jnp.exp2((s - jnp.max(s, axis=1, keepdims=True)) * GROW)
                 grads = dp[j, at, :]
                 inv = 1.0 / jnp.sum(e, axis=1, keepdims=True)
@@ -151,8 +156,8 @@
 
             def first_pass(t, c):
                 start = tile_at(j, t)
-                more[...] = bias_tile(dl, docs, span, wins[j][0], wins[j][1] - t * TILE)
-                dp[t] = mm(qs[j], ks[pl.ds(start, TILE), :], NT)
+                more[...] = tile_mask(dl, wins[j][0], wins[j][1] - (t + 1) * TILE, more.shape, 0)
+                dp[t] = mm(qs[j, :, 0:DH], ks[pl.ds(start, TILE), :], NT)
                 for at in head_rows:
                     s = dp[t, at, :] + more[...]
                     sc[t, at, :] = s
@@ -183,17 +188,20 @@
             lax.fori_loop(0, count, second_pass, 0)
             lax.fori_loop(0, count, third_pass, 0)
 
-    for m in range(n):
-        for j in range(spans_own):
-            at = place(m, j)
-            to = slice(j * span, (j + 1) * span)
-            parts[m][to, 0:DH] = (dk[pl.ds(at, span), :] * SCALE).astype(parts[m].dtype)
-            parts[m][to, DH : 2 * DH] = dv[pl.ds(at, span), :].astype(parts[m].dtype)
+    for m in range(1, n):
+        for j in range(spans_own):
+            take_block(parts[m - 1], dk, dv, place(m, j), j, span)
+
+
+def take_block(out, dk, dv, at, j, span):
+    to = slice(j * span, (j + 1) * span)
+    out[to, 0:DH] = (dk[pl.ds(at, span), :] * SCALE).astype(out.dtype)
+    out[to, DH : 2 * DH] = dv[pl.ds(at, span), :].astype(out.dtype)
 
 
 def back_kernel(n, heads, span, spans_all, docs, info, *refs):
-    pb, db, kw, vw, oa, qa, att_ref, dq_ref = refs
-    unused, wins, short = unpack(info, n, span, spans_all, docs)
+    pb, db, kw, vw, oa, qa, dk, dv, att_ref, dq_ref, mine = refs
+    spots, wins, short = unpack(info, n, span, spans_all, docs)
     spans_own = len(wins)
 
     def store(j, o, dq):
@@ -206,12 +214,15 @@
     @pl.when(short)
     def _():
         for j in range(spans_own):
-            store(j, mm(pb[j], vw[j], NN), mm(db[j], kw[j], NN))
+            store(j, mm(pb[j], vw[j], NN), mm(db[j], kw[j, :, 0:DH], NN))
 
     @pl.when(jnp.logical_not(short))
     def _():
         for j in range(spans_own):
             store(j, oa[j], qa[j])
+
+    for j in range(spans_own):
+        take_block(mine, dk, dv, pl.multiple_of(spots[j], 16), j, span)
 
 
 def merge_kernel(a, b, c, key_ref, value_ref):
@@ -230,6 +241,7 @@
     seq = tok * n
     span = seq // spans_all
     rows = heads * span
+    lanes = DH + 128 * (-(-span // 128))
     tiles = max(spans_own, -(-seq // TILE))
     bits = [1 << b for b in range(n.bit_length() - 1)]
     bf, f32 = jnp.bfloat16, jnp.float32
@@ -252,14 +264,16 @@
     def back(*refs):
         back_kernel(*sizes, *refs)
 
-    part = [S((tok, 2 * DH), bf if m % 2 else f32) for m in range(n)]
+    part = [S((tok, 2 * DH), bf if m % 2 else f32) for m in range(1, n)]
     middle = [
         S((spans_own, rows, TILE), bf),
         S((spans_own, rows, TILE), bf),
-        S((spans_own, TILE, DH), bf),
+        S((spans_own, TILE, lanes), bf),
         S((spans_own, TILE, DH), bf),
         S((spans_own, rows, DH), f32),
         S((spans_own, rows, DH), f32),
+        S((TILE + seq, DH), f32),
+        S((TILE + seq, DH), f32),
     ]
     def side(a, b, axis):
         before = [(0, 0)] * a.ndim
@@ -274,31 +288,32 @@
         for m in list(kv):
             with jax.named_scope("hop%d" % bit):
                 kv[m | bit] = swap(kv[m], bit)
-    qs, gs, bias, info, qt, gt = pl.pallas_call(
+    qs, gs, mask, info, qt, gt, zk, zv = pl.pallas_call(
         prepare,
         out_shape=[
+            S((spans_own, rows, lanes), bf),
             S((spans_own, rows, DH), bf),
-            S((spans_own, rows, DH), bf),
-            S((spans_own, span, TILE), f32),
+            S((spans_own, TILE, lanes - DH), bf),
             S((8, 128 * -(-(spans_all + 2 * spans_own + docs) // 128)), jnp.int32),
             S((spans_own, DH, rows), bf),
             S((spans_own, DH, rows), bf),
+            S((TILE + seq, DH), f32),
+            S((TILE + seq, DH), f32),
         ],
         in_specs=[sm, vm],
-        out_specs=[vm] * 6,
+        out_specs=[vm] * 8,
         compiler_params=pltpu.CompilerParams(vmem_limit_bytes=8 << 20),
         name="prepare",
     )(meta, side(queries, out_grad, 0))
     res = pl.pallas_call(
         front,
         out_shape=part + middle,
-        in_specs=[vm] * (6 + n),
-        out_specs=[vm] * (n + 6),
+        in_specs=[vm] * (8 + n),
+        out_specs=[vm] * (n + 7),
+        input_output_aliases={6: n + 5, 7: n + 6},
         scratch_shapes=[
             V((TILE + seq, DH), bf),
             V((TILE + seq, DH), bf),
-            V((TILE + seq, DH), f32),
-            V((TILE + seq, DH), f32),
             V((tiles, rows, TILE), f32),
             V((tiles, rows, TILE), f32),
             V((rows, DH), f32),
@@ -308,17 +323,19 @@
         ],
         compiler_params=pltpu.CompilerParams(vmem_limit_bytes=(16 + 3 * tiles) << 20),
         name="front",
-    )(info, qs, gs, bias, qt, gt, *[kv[m] for m in range(n)])
-    attended, query_grad = pl.pallas_call(
+    )(info, qs, gs, mask, qt, gt, zk, zv, *[kv[m] for m in range(n)])
+    attended, query_grad, mine = pl.pallas_call(
         back,
-        out_shape=[S((tok, width), bf), S((tok, width), bf)],
-        in_specs=[vm] * 7,
-        out_specs=[vm, vm],
+        out_shape=[S((tok, width), bf), S((tok, width), bf), S((tok, 2 * DH), f32)],
+        in_specs=[vm] * 9,
+        out_specs=[vm] * 3,
         compiler_params=pltpu.CompilerParams(vmem_limit_bytes=16 << 20),
         name="back",
-    )(info, *res[n:])
-
-    held = {m: [res[m]] for m in range(n)}
+    )(info, *res[n - 1 :])
+
+    held = {0: [mine]}
+    for m in range(1, n):
+        held[m] = [res[m - 1]]
     for bit in bits:
         for m in sorted(held, reverse=True):
             if m & bit:

time: 18.2 us -> 18.2 us (level)
  transfers between devices with their start and end apart: 6 -> 6, of which waited for: 4 -> 4; matrix products, arithmetic and copies ran while one was open for 7% -> 7% of each run, Pallas kernels for 14% -> 15%
where the time goes in v4:
time: 18.2 us; the launch traced here: 18 us
  Pallas kernels  5.61 us (31%)
  starting transfers between devices  5.5 us (30%)
  waiting for transfers between devices  4.12 us (23%)
  other arithmetic  2.11 us (12%)
  between operations  0.69 us (4%)
    ppermute x6, starting transfers between devices, swap(): return lax.ppermute(x, 'ctx', [(i, i ^ m) for i in range(n)])  5.5 us
    ppermute x6, waiting for transfers between devices, swap(): return lax.ppermute(x, 'ctx', [(i, i ^ m) for i in range(n)])  4.12 us
    pallas_call x1, Pallas kernels, local(): pl.pallas_call(front, out_shape=part + middle, in_specs=[vm] * (8 + n), o...  2.22 us
    add x3, other arithmetic, side(): return jnp.pad(a, after) + jnp.pad(b, before)  2.09 us
    pallas_call x1, Pallas kernels, local(): pl.pallas_call(back, out_shape=[S((tok, width), bf), S((tok, width), bf),...  1.77 us
    pallas_call x1, Pallas kernels, local(): pl.pallas_call(prepare, out_shape=[S((spans_own, rows, lanes), bf), S((sp...  0.96 us
    pallas_call x1, Pallas kernels, local(): pl.pallas_call(merge_kernel, out_shape=[half, half], in_specs=[vm] * 3, o...  0.66 us
  transfers between devices with their start and end apart: 6, of which 4 were waited for; matrix products, arithmetic and copies ran while one was open for 7% of the time, Pallas kernels for 15%

profile of v4, /device:TPU:0, one launch (start us, length us, event | category | flops | bytes accessed | tf_op | source)
XLA Modules:
  0.0 18.0 jit_solution(1426821742415557069)
XLA Ops:
  0.6 0.0 copy-start
  0.6 0.0 copy-start.1
  0.7 0.8 %pad_add_fusion.1.refs_8_ = bf16[192,256]{1,0:T(8,128)(2,1)S(1)} fusion(bf16[192,128]{1,0:T(8,128)(2,1)} %param.8, bf16[192,128]{1,0:T(8,128)(2,1)} %param.7), kind=kLoop, calls=%fused_computation.2 | loop fusion | flops 196608 | bytes 196608 | tf_op jit(solution)/shard_map/add | solution.py:283
  1.5 3.0 %collective-permute-start.1 = (bf16[192,256]{1,0:T(8,128)(2,1)S(1)}, bf16[192,256]{1,0:T(8,128)(2,1)S(1)}, u32[]{:S(2)}, u32[]{:S(2)}) collective-permute-start(bf16[192,256]{1,0:T(8,128)(2,1)S(1)} %pad_add_fusion.1.refs_8_), channel_id=1, source_target_pairs={{0,16},{8,24},{16,0},{24,8},{1,17},{9,25},{17,1},{25,9},{2,18},{10... | collective-permute-start | bytes 294920 | tf_op jit(solution)/shard_map/hop2/ppermute | solution.py:250
  4.5 0.0 collective-permute-start
  4.5 1.2 %pad_add_fusion.refs_1_ = bf16[384,1024]{1,0:T(8,128)(2,1)S(1)} fusion(bf16[192,1024]{1,0:T(8,128)(2,1)} %param.9, bf16[192,1024]{1,0:T(8,128)(2,1)} %param.6), kind=kLoop, calls=%fused_computation | loop fusion | flops 1572864 | bytes 1572864 | tf_op jit(solution)/shard_map/add | solution.py:283
  5.7 1.6 %collective-permute-done.1.refs_10_ = bf16[192,256]{1,0:T(8,128)(2,1)S(1)} collective-permute-done((bf16[192,256]{1,0:T(8,128)(2,1)S(1)}, bf16[192,256]{1,0:T(8,128)(2,1)S(1)}, u32[]{:S(2)}, u32[]{:S(2)}) %collective-permute-start.1) | collective-permute-done | bytes 98336 | tf_op jit(solution)/shard_map/hop2/ppermute | solution.py:250
  7.3 0.0 collective-permute-start.2
  7.3 0.0 copy-done
  7.3 0.0 copy-done.1
  7.3 0.1 pad_add_fusion.2.refs_0_
  7.4 1.0 %prepare.1 = (bf16[2,768,256]{2,1,0:T(8,128)(2,1)S(1)}, bf16[2,768,128]{2,1,0:T(8,128)(2,1)S(1)}, bf16[2,384,128]{2,1,0:T(8,128)(2,1)S(1)}, s32[8,128]{1,0:T(8,1...) custom-call(s32[14]{0:T(128)S(1)} %pad_add_fusion.2.refs_0_, ...), custom_call_target="tpu_custom_call" | custom-call | tf_op jit(solution)/shard_map/prepare/pallas_call | solution.py:291
  8.4 0.0 collective-permute-done.refs_9_
  8.4 0.2 %collective-permute-done.2.refs_11_ = bf16[192,256]{1,0:T(8,128)(2,1)S(1)} collective-permute-done((bf16[192,256]{1,0:T(8,128)(2,1)S(1)}, bf16[192,256]{1,0:T(8,128)(2,1)S(1)}, u32[]{:S(2)}, u32[]{:S(2)}) %collective-permute-start.2) | collective-permute-done | bytes 98336 | tf_op jit(solution)/shard_map/hop1/ppermute | solution.py:250
  8.6 2.2 %front.1 = (bf16[192,256]{1,0:T(8,128)(2,1)S(1)}, f32[192,256]{1,0:T(8,128)S(1)}, bf16[192,256]{1,0:T(8,128)(2,1)S(1)}, bf16[2,768,384]{2,1,0:T(8,128)(2,1)S(1)}...) custom-call(s32[8,128]{1,0:T(8,128)S(1)} %get-tuple-element.28.refs_, ...), custom_call_target="tpu_custom_call", output_to_operand_aliasing={{9}: (6, {}), {10}: (7, {})} | custom-call | tf_op jit(solution)/shard_map/front/pallas_call | solution.py:308
  10.9 0.4 %collective-permute-start.4 = (bf16[192,256]{1,0:T(8,128)(2,1)S(1)}, bf16[192,256]{1,0:T(8,128)(2,1)S(1)}, u32[]{:S(2)}, u32[]{:S(2)}) collective-permute-start(bf16[192,256]{1,0:T(8,128)(2,1)S(1)} %get-tuple-element.49), channel_id=1, source_target_pairs={{0,8},{8,0},{16,24},{24,16},{1,9},{9,1},{17,25},{25,17},{2,10},{10... | collective-permute-start | bytes 294920 | tf_op jit(solution)/shard_map/ppermute | solution.py:250
  11.2 0.2 %collective-permute-start.3 = (bf16[192,256]{1,0:T(8,128)(2,1)S(1)}, bf16[192,256]{1,0:T(8,128)(2,1)S(1)}, u32[]{:S(2)}, u32[]{:S(2)}) collective-permute-start(bf16[192,256]{1,0:T(8,128)(2,1)S(1)} %get-tuple-element.47), channel_id=1, source_target_pairs={{0,8},{8,0},{16,24},{24,16},{1,9},{9,1},{17,25},{25,17},{2,10},{10... | collective-permute-start | bytes 294920 | tf_op jit(solution)/shard_map/ppermute | solution.py:250
  11.4 0.8 %collective-permute-done.4 = bf16[192,256]{1,0:T(8,128)(2,1)S(1)} collective-permute-done((bf16[192,256]{1,0:T(8,128)(2,1)S(1)}, bf16[192,256]{1,0:T(8,128)(2,1)S(1)}, u32[]{:S(2)}, u32[]{:S(2)}) %collective-permute-start.4) | collective-permute-done | bytes 98336 | tf_op jit(solution)/shard_map/ppermute | solution.py:250
  12.3 1.9 %collective-permute-start.5 = (bf16[192,256]{1,0:T(8,128)(2,1)S(1)}, bf16[192,256]{1,0:T(8,128)(2,1)S(1)}, u32[]{:S(2)}, u32[]{:S(2)}) collective-permute-start(bf16[192,256]{1,0:T(8,128)(2,1)S(1)} %add_convert_fusion), channel_id=1, source_target_pairs={{0,16},{8,24},{16,0},{24,8},{1,17},{9,25},{17,1},{25,9},{2,18},{10... | collective-permute-start | bytes 294920 | tf_op jit(solution)/shard_map/ppermute | solution.py:250
  14.1 1.8 %back.1 = (bf16[192,1024]{1,0:T(8,128)(2,1)}, bf16[192,1024]{1,0:T(8,128)(2,1)}, f32[192,256]{1,0:T(8,128)S(1)}) custom-call(s32[8,128]{1,0:T(8,128)S(1)} %get-tuple-element.28.refs_0_, bf16[2,768,384]{2,1,0:T(8,128)(2,1)S(1)} %get-tuple-element.36.refs_1_, bf16[2,768,384]{2,1,0:T(8,128)(2,1)S(1)} %get-tuple-element.37.refs_2_, ...), custom_call_target="tpu_custom_call" | custom-call | tf_op jit(solution)/shard_map/back/pallas_call | solution.py:327
  15.9 0.0 collective-permute-done.3.b
  15.9 1.5 %collective-permute-done.5.c = bf16[192,256]{1,0:T(8,128)(2,1)S(1)} collective-permute-done((bf16[192,256]{1,0:T(8,128)(2,1)S(1)}, bf16[192,256]{1,0:T(8,128)(2,1)S(1)}, u32[]{:S(2)}, u32[]{:S(2)}) %collective-permute-start.5) | collective-permute-done | bytes 98336 | tf_op jit(solution)/shard_map/ppermute | solution.py:250
  17.4 0.7 %merge.1 = (bf16[192,128]{1,0:T(8,128)(2,1)}, bf16[192,128]{1,0:T(8,128)(2,1)}) custom-call(f32[192,256]{1,0:T(8,128)S(1)} %get-tuple-element.46.a, bf16[192,256]{1,0:T(8,128)(2,1)S(1)} %collective-permute-done.3.b, bf16[192,256]{1,0:T(8,128)(2,1)S(1)} %collective-permute-done.5.c), custom_call_target="tpu_custom_call" | custom-call | tf_op jit(solution)/shard_map/merge/pallas_call | solution.py:351
  (1 shorter events, 0.0 us)
Async XLA Ops:
  0.6 6.7 %copy-start = (s32[6]{0:T(128)S(1)}, s32[6]{0:T(128)}, u32[]{:S(2)}) copy-start(s32[6]{0:T(128)} %param.11) | copy-start | bytes 76
  0.6 6.7 %copy-start.1 = (s32[8]{0:T(128)S(1)}, s32[8]{0:T(128)}, u32[]{:S(2)}) copy-start(s32[8]{0:T(128)} %param.10) | copy-start | bytes 100
  1.5 5.8 %collective-permute-start.1 = (bf16[192,256]{1,0:T(8,128)(2,1)S(1)}, bf16[192,256]{1,0:T(8,128)(2,1)S(1)}, u32[]{:S(2)}, u32[]{:S(2)}) collective-permute-start(bf16[192,256]{1,0:T(8,128)(2,1)S(1)} %pad_add_fusion.1.refs_8_), channel_id=1, source_target_pairs={{0,16},{8,24},{16,0},{24,8},{1,17},{9,25},{17,1},{25,9},{2,18},{10... | collective-permute-start | bytes 294920 | tf_op jit(solution)/shard_map/hop2/ppermute | solution.py:250
  4.5 3.9 %collective-permute-start = (bf16[192,256]{1,0:T(8,128)(2,1)S(1)}, bf16[192,256]{1,0:T(8,128)(2,1)S(1)}, u32[]{:S(2)}, u32[]{:S(2)}) collective-permute-start(bf16[192,256]{1,0:T(8,128)(2,1)S(1)} %pad_add_fusion.1.refs_8_), channel_id=1, source_target_pairs={{0,8},{8,0},{16,24},{24,16},{1,9},{9,1},{17,25},{25,17},{2,10},{10... | collective-permute-start | bytes 294920 | tf_op jit(solution)/shard_map/hop1/ppermute | solution.py:250
  7.3 1.3 %collective-permute-start.2 = (bf16[192,256]{1,0:T(8,128)(2,1)S(1)}, bf16[192,256]{1,0:T(8,128)(2,1)S(1)}, u32[]{:S(2)}, u32[]{:S(2)}) collective-permute-start(bf16[192,256]{1,0:T(8,128)(2,1)S(1)} %collective-permute-done.1.refs_10_), channel_id=1, source_target_pairs={{0,8},{8,0},{16,24},{24,16},{1,9},{9,1},{17,25},{25,17},{2,10},{10... | collective-permute-start | bytes 294920 | tf_op jit(solution)/shard_map/hop1/ppermute | solution.py:250
  10.9 1.4 %collective-permute-start.4 = (bf16[192,256]{1,0:T(8,128)(2,1)S(1)}, bf16[192,256]{1,0:T(8,128)(2,1)S(1)}, u32[]{:S(2)}, u32[]{:S(2)}) collective-permute-start(bf16[192,256]{1,0:T(8,128)(2,1)S(1)} %get-tuple-element.49), channel_id=1, source_target_pairs={{0,8},{8,0},{16,24},{24,16},{1,9},{9,1},{17,25},{25,17},{2,10},{10... | collective-permute-start | bytes 294920 | tf_op jit(solution)/shard_map/ppermute | solution.py:250
  11.2 4.7 %collective-permute-start.3 = (bf16[192,256]{1,0:T(8,128)(2,1)S(1)}, bf16[192,256]{1,0:T(8,128)(2,1)S(1)}, u32[]{:S(2)}, u32[]{:S(2)}) collective-permute-start(bf16[192,256]{1,0:T(8,128)(2,1)S(1)} %get-tuple-element.47), channel_id=1, source_target_pairs={{0,8},{8,0},{16,24},{24,16},{1,9},{9,1},{17,25},{25,17},{2,10},{10... | collective-permute-start | bytes 294920 | tf_op jit(solution)/shard_map/ppermute | solution.py:250
  12.3 5.1 %collective-permute-start.5 = (bf16[192,256]{1,0:T(8,128)(2,1)S(1)}, bf16[192,256]{1,0:T(8,128)(2,1)S(1)}, u32[]{:S(2)}, u32[]{:S(2)}) collective-permute-start(bf16[192,256]{1,0:T(8,128)(2,1)S(1)} %add_convert_fusion), channel_id=1, source_target_pairs={{0,16},{8,24},{16,0},{24,8},{1,17},{9,25},{17,1},{25,9},{2,18},{10... | collective-permute-start | bytes 294920 | tf_op jit(solution)/shard_map/ppermute | solution.py:250
